TPU v7x, 128 devices: a whole 4x4x4 slice. The times are simulated.
128 devices in a mesh: branch: 2 (over core), seq: 32 (over z, y, x_lo), mp: 2 (over x_hi).
Axes of the slice: x: 4 (x_hi: 2, x_lo: 2; x = x_hi * 2 + x_lo), y: 4, z: 4, core: 2. Of those that a mesh axis runs over, the one named last changes fastest.
Arguments:
- tokens: bfloat16 [8192, 4096], P('seq', 'mp'), may hold values from -6 to 6
- light_in: bfloat16 [4096, 2048], P(None, ('branch', 'mp')), may hold values from -0.09375 to 0.09375
- light_out: bfloat16 [2048, 4096], P(('branch', 'mp')), may hold values from -0.1875 to 0.1875
- heavy_in: bfloat16 [4096, 16384], P(None, ('branch', 'seq', 'mp')), may hold values from -0.09375 to 0.09375
- heavy_out: bfloat16 [16384, 4096], P(('branch', 'seq', 'mp')), may hold values from -0.1875 to 0.1875
- route_index: int32 [32, 32], P('seq'), may hold values from 0 to 255, as said below
- route_count: int32 [32], P('seq'), may hold values from 1 to 32, as said below
- route_gate: float32 [32, 32], P('seq'), may hold values from 0.25 to 2
- cotangent: bfloat16 [8192, 4096], P('seq', 'mp'), may hold values from -6 to 6
Outputs:
- mixed: bfloat16 [8192, 4096], P('seq', ('branch', 'mp'))
- grad_heavy_in: bfloat16 [4096, 16384], P(None, ('branch', 'seq', 'mp'))
- grad_heavy_out: bfloat16 [16384, 4096], P(('branch', 'seq', 'mp'))
Inputs may be any that keep to these rules, and one draw needn't show every extreme that they name: `route_index`: each row holds 32 distinct positions of its shard. The first route_count[s] slots of shard s are live; some shard has all 32 slots live.
All inputs are finite; a program needn't handle non-finite values.
Results may differ from a plain program's by a relative error of at most 0.008.
Values may be sent and summed in bfloat16 or wider, within the bound.
No kernel may reach another device: no remote copies, remote signals or barrier semaphores. Data moves between devices by JAX's collectives and lax.ppermute only.
A program may use at most 128 MiB of HBM per device.

v0:
```python
import itertools

import jax
import jax.numpy as jnp
from jax import lax
from jax.experimental import pallas as pl
from jax.sharding import Mesh, PartitionSpec as P


root_coef = 0.7978845608
cubic_coef = 0.044715

swap = [(0, 1), (1, 0)]
axes = ("b", "z", "y", "xl", "xh")
sizes = (2, 4, 4, 2, 2)


def gelu_tanh(values):
    inner = root_coef * (values + cubic_coef * values * values * values)
    return 0.5 * values * (1.0 + jnp.tanh(inner))


def gelu_slope(values):
    tangent = jnp.tanh(root_coef * (values + cubic_coef * values * values * values))
    return 0.5 * (1.0 + tangent) + 0.5 * values * (1.0 - tangent * tangent) * root_coef * (
        1.0 + 3.0 * cubic_coef * values * values
    )


def dot(left, right):
    return jnp.dot(left, right, preferred_element_type=jnp.float32)


def general(left, right, left_dims, right_dims):
    return lax.dot_general(
        left, right, ((left_dims, right_dims), ((), ())), preferred_element_type=jnp.float32
    )


def part(x, index, size, dim):
    return lax.dynamic_slice_in_dim(x, index * size, size, axis=dim)


def ordered(first, mine, other, dim):
    return jnp.where(
        first, jnp.concatenate([mine, other], dim), jnp.concatenate([other, mine], dim)
    )


def number(place):
    result = 0
    for at, size in zip(place, sizes):
        result = result * size + at % size
    return result


def moved(x, step):
    places = itertools.product(*(range(size) for size in sizes))
    return lax.ppermute(x, axes, [(number(p), number(step(*p))) for p in places])


def second(by):
    return lambda b, z, y, xl, xh: (b, z + by * b, y + by * (1 - b), xl, xh)


def third(by):
    return lambda b, z, y, xl, xh: (b, z + by * (1 - b), y + by * b, xl, xh)


def rows_product(left, tiles):
    return lax.dot_general(
        left, tiles, (((0,), (0,)), ((), ())), preferred_element_type=jnp.float32
    )


def grad_out_of(hidden, back, tile=512):
    sides, rows, width = back.shape
    units = hidden.shape[1]
    per_side = width // tile

    def kernel(hidden_ref, back_ref, out_ref):
        out_ref[...] = rows_product(hidden_ref[...], back_ref[0]).astype(out_ref.dtype)

    return pl.pallas_call(
        kernel,
        grid=(sides * per_side,),
        in_specs=[
            pl.BlockSpec((rows, units), lambda i: (0, 0)),
            pl.BlockSpec((1, rows, tile), lambda i: (i // per_side, 0, i % per_side)),
        ],
        out_specs=pl.BlockSpec((units, tile), lambda i: (0, i)),
        out_shape=jax.ShapeDtypeStruct((units, sides * width), jnp.bfloat16),
        cost_estimate=pl.CostEstimate(
            flops=2 * rows * units * sides * width,
            bytes_accessed=2 * (sides * rows * width + units * sides * width),
            transcendentals=0,
        ),
    )(hidden, back)


def grad_in_of(sheets, slope, tile=512):
    tall, features = sheets[0].shape
    rows, units = slope.shape

    def kernel(*refs):
        slope_ref, out_ref = refs[-2:]
        tiles = jnp.concatenate([ref[...] for ref in refs[:-2]], axis=0)
        out_ref[...] = rows_product(slope_ref[...], tiles).T.astype(out_ref.dtype)

    return pl.pallas_call(
        kernel,
        grid=(features // tile,),
        in_specs=[pl.BlockSpec((tall, tile), lambda i: (0, i)) for _ in sheets]
        + [pl.BlockSpec((rows, units), lambda i: (0, 0))],
        out_specs=pl.BlockSpec((tile, units), lambda i: (i, 0)),
        out_shape=jax.ShapeDtypeStruct((features, units), jnp.bfloat16),
        cost_estimate=pl.CostEstimate(
            flops=2 * rows * units * features,
            bytes_accessed=2 * (rows * features + units * features),
            transcendentals=0,
        ),
    )(*sheets, slope)


def per_device(
    tokens,
    light_in,
    light_out,
    heavy_in,
    heavy_out,
    route_index,
    route_count,
    route_gate,
    cotangent,
):
    core = lax.axis_index("b")
    side = lax.axis_index("xh")
    low = lax.axis_index("xl")
    at_y = lax.axis_index("y")
    at_z = lax.axis_index("z")
    rows, width = tokens.shape
    slots = route_index.shape[1]
    half = slots // 2
    block = heavy_out.shape[1] // 4
    units = heavy_out.shape[0]

    positions = route_index[0]
    live_slots = jnp.arange(slots, dtype=jnp.int32) < route_count[0]
    row_scale = jnp.where(live_slots, route_gate[0], jnp.zeros_like(route_gate[0]))
    own_positions = part(positions, core, half, 0)
    own_scale = part(row_scale, core, half, 0)
    picked = jnp.take(tokens, own_positions, axis=0, mode="clip")
    picked, later_positions = lax.optimization_barrier((picked, own_positions))
    back = jnp.take(cotangent, later_positions, axis=0, mode="clip").astype(jnp.float32)
    back = (back * own_scale[:, None]).astype(jnp.bfloat16)
    back = lax.all_gather(back, ("xh", "xl", "y", "z", "b"), axis=0, tiled=True)
    back = back.reshape(2, back.shape[0] // 2, width)

    over_side = moved(picked, lambda b, z, y, xl, xh: (b, z, y, xl, xh + 1))
    over_low = moved(picked, lambda b, z, y, xl, xh: (b, z, y, xl + 1, xh))
    over_both = moved(picked, lambda b, z, y, xl, xh: (b, z, y, xl + 1, xh + 1))
    plane = ordered(
        low == 0,
        ordered(side == 0, picked, over_side, 1),
        ordered(side == 0, over_low, over_both, 1),
        0,
    )
    plane, later_tokens = lax.optimization_barrier((plane, tokens))
    sheet = jnp.concatenate([plane] + [moved(plane, second(-k)) for k in (1, 2, 3)], axis=0)
    sheet, later_out = lax.optimization_barrier((sheet, heavy_out))
    after = moved(sheet, third(-1))
    before = moved(sheet, third(1))
    cut = sheet.shape[0] // 2
    facing = [moved(after[:cut], third(-1)), moved(before[cut:], third(1))]
    facing = jnp.concatenate(facing, axis=0)
    sheets = (sheet, after, facing, before)

    chip_in = jnp.concatenate([heavy_in, lax.ppermute(heavy_in, "b", swap)], axis=1)
    kept = jnp.concatenate([part(later_out, 2 * k + side, block, 1) for k in (0, 1)], axis=1)
    given = [part(later_out, 2 * k + 1 - side, block, 1) for k in (0, 1)]
    given = jnp.concatenate(given, axis=1)
    got_out = lax.ppermute(given, "xh", swap)
    kept_other = lax.ppermute(kept, "b", swap)
    got_other = lax.ppermute(got_out, "b", swap)
    group_weight = jnp.concatenate([kept, kept_other, got_out, got_other], axis=0)

    sent = part(later_tokens, core, rows // 2, 0)
    got = lax.ppermute(sent, "xh", swap)
    other = ordered(core == 0, got, lax.ppermute(got, "b", swap), 0)
    whole = ordered(side == 0, tokens, other, 1)
    light_hidden = gelu_tanh(dot(whole, light_in)).astype(jnp.bfloat16)
    theirs = dot(light_hidden, part(light_out, 1 - core, width, 1))
    mine = dot(light_hidden, part(light_out, core, width, 1))
    chip_terms = mine + lax.ppermute(theirs, "b", swap)
    light_kept = part(chip_terms, side, block, 1)
    light_given = part(chip_terms, 1 - side, block, 1).astype(jnp.bfloat16)

    pre_acts = []
    for name, one in zip(("pre_own", "pre_near", "pre_facing", "pre_near"), sheets):
        pre = dot(one, chip_in)
        if name != "pre_facing":
            pre = lax.optimization_barrier(pre)
        pre_acts.append(pre)
    tall = sheet.shape[0]
    early = jnp.concatenate([pre_acts[1], pre_acts[3], pre_acts[0]], axis=0)
    early = gelu_tanh(early).astype(jnp.bfloat16)
    early = jnp.concatenate([early, lax.ppermute(early, "xh", swap)], axis=1)
    late = gelu_tanh(pre_acts[2]).astype(jnp.bfloat16)
    across = lax.ppermute(late, "xh", swap)
    late = jnp.concatenate([late, across], axis=1)
    near = dot(early[: 2 * tall], group_weight).astype(jnp.bfloat16)
    far = dot(late, group_weight).astype(jnp.bfloat16)
    light_got = lax.ppermute(light_given, "xh", swap)
    light_share = light_kept + light_got.astype(jnp.float32)
    own = dot(early[2 * tall :], group_weight)
    from_before = moved(near[:tall], third(1))
    from_after = moved(near[tall:], third(-1))
    from_facing = moved(far, third(2))
    for one in (from_before, from_after, from_facing):
        own = own + one.astype(jnp.float32)
    strip = plane.shape[0]
    leaving = own.astype(jnp.bfloat16)
    total = own[:strip]
    strips = [moved(leaving[k * strip : (k + 1) * strip], second(k)) for k in (1, 2, 3)]
    for one in strips:
        total = total + one.astype(jnp.float32)
    count = 4 * tall
    r = jnp.arange(count, dtype=jnp.int32)
    r_slot, r_z, r_y, r_low = r % half, r // half % 4, r // (4 * half) % 4, r // (16 * half)
    turn_z, turn_y = (r_z - at_z) % 4, (r_y - at_y) % 4
    inner = r_low * half + r_slot
    place = jnp.where(core == 0, turn_z * 4 + turn_y, turn_y * 4 + turn_z) * (2 * half) + inner
    place_other = (
        jnp.where(core == 0, turn_y * 4 + turn_z, turn_z * 4 + turn_y) * (2 * half) + inner
    )
    choice = (place[:, None] == r[None, :]).astype(jnp.bfloat16)

    pre_act = jnp.concatenate(pre_acts, axis=0)
    pre_rows = jnp.dot(
        choice.astype(jnp.float32),
        pre_act,
        precision=lax.Precision.HIGHEST,
        preferred_element_type=jnp.float32,
    )

    def both_cores(own, theirs):
        pieces = [own.reshape(-1, 1, half, units), theirs.reshape(-1, 1, half, units)]
        return ordered(core == 0, pieces[0], pieces[1], 1).reshape(2 * count, units)

    pre_all = both_cores(pre_rows[:, :units], lax.ppermute(pre_rows[:, units:], "b", swap))
    hidden_all = gelu_tanh(pre_all).astype(jnp.bfloat16)
    slope = general(back[0], heavy_out[:, :width], (1,), (1,)) + general(
        back[1], heavy_out[:, width:], (1,), (1,)
    )
    slope = (slope * gelu_slope(pre_all)).astype(jnp.bfloat16)
    grad_out = grad_out_of(hidden_all, back)
    places = jnp.stack([place, place_other + count])
    places = jnp.where(core == 0, places, places[::-1])
    places = places.reshape(2, -1, half).swapaxes(0, 1).reshape(-1)
    wide = jnp.arange(2 * count, dtype=jnp.int32)
    back_choice = (wide[:, None] == places[None, :]).astype(jnp.bfloat16)
    slope_rows = dot(back_choice, slope).astype(jnp.bfloat16)
    total, slope_rows, grad_out = lax.optimization_barrier((total, slope_rows, grad_out))
    homed = part(total, low, half, 0) + lax.ppermute(
        part(total, 1 - low, half, 0).astype(jnp.bfloat16), "xl", swap
    ).astype(jnp.float32)
    theirs_sheets = [lax.ppermute(one, "b", swap) for one in sheets]
    grad_in = grad_in_of(list(sheets) + theirs_sheets, slope_rows)
    swapped = lax.ppermute(part(homed, 1 - core, block, 1), "b", swap)
    heavy_share = ordered(core == 0, part(homed, core, block, 1), swapped, 0) * row_scale[:, None]
    naming = (jnp.arange(rows, dtype=jnp.int32)[:, None] == positions[None, :]).astype(jnp.float32)
    spread = jnp.dot(
        naming, heavy_share, precision=lax.Precision.HIGHEST, preferred_element_type=jnp.float32
    )
    mixed = (light_share + spread).astype(jnp.bfloat16)


    return (mixed, grad_in, grad_out)


def solution(mesh):
    split = Mesh(mesh.devices.reshape(*sizes), axes)
    seq = ("z", "y", "xl")
    units = axes
    in_specs = (
        P(seq, "xh"),
        P(None, ("b", "xh")),
        P(("b", "xh"), None),
        P(None, units),
        P(units, None),
        P(seq, None),
        P(seq),
        P(seq, None),
        P(seq, "xh"),
    )
    out_specs = (
        P(seq, ("b", "xh")),
        P(None, units),
        P(units, None),
    )

    return jax.shard_map(
        per_device, mesh=split, in_specs=in_specs, out_specs=out_specs, check_vma=False
    )
```

profile of v0, /device:TPU:0, one launch (start us, length us, event | category | flops | bytes accessed | tf_op | source)
XLA Modules:
  0.0 171.7 jit_solution(9014369390207577786)
XLA Ops:
  12.9 3.2 %collective-permute-start = (bf16[16,2048]{1,0:T(8,128)(2,1)S(1)}, bf16[16,2048]{1,0:T(8,128)(2,1)S(1)}, u32[]{:S(2)}, u32[]{:S(2)}) collective-permute-start(bf16[16,2048]{1,0:T(8,128)(2,1)S(1)} %gather_fusion), channel_id=1, source_target_pairs={{0,1},{1,0},{2,3},{3,2},{4,5},{5,4},{6,7},{7,6},{8,9},{9,8},{10,11... | collective-permute-start | bytes 196616 | tf_op jit(solution)/shard_map/ppermute | solution.py:59
  22.2 3.1 %collective-permute-start.7 = (bf16[32,4096]{1,0:T(8,128)(2,1)S(1)}, bf16[32,4096]{1,0:T(8,128)(2,1)}, u32[]{:S(2)}, u32[]{:S(2)}) collective-permute-start(bf16[32,4096]{1,0:T(8,128)(2,1)S(1)} %maximum_select_fusion.6), channel_id=1, source_target_pairs={{0,12},{1,13},{2,14},{3,15},{4,0},{5,1},{6,2},{7,3},{8,4},{9,5},{1... | collective-permute-start | bytes 786440 | tf_op jit(solution)/shard_map/ppermute | solution.py:59
  28.6 3.8 %collective-permute-done.7 = bf16[32,4096]{1,0:T(8,128)(2,1)} collective-permute-done((bf16[32,4096]{1,0:T(8,128)(2,1)S(1)}, bf16[32,4096]{1,0:T(8,128)(2,1)}, u32[]{:S(2)}, u32[]{:S(2)}) %collective-permute-start.7) | collective-permute-done | bytes 262176 | tf_op jit(solution)/shard_map/ppermute | solution.py:59
  33.5 3.0 %collective-permute-done.9 = bf16[32,4096]{1,0:T(8,128)(2,1)} collective-permute-done((bf16[32,4096]{1,0:T(8,128)(2,1)S(1)}, bf16[32,4096]{1,0:T(8,128)(2,1)}, u32[]{:S(2)}, u32[]{:S(2)}) %collective-permute-start.9) | collective-permute-done | bytes 262176 | tf_op jit(solution)/shard_map/ppermute | solution.py:59
  36.5 2.2 %pad_maximum_fusion.1.refs_0_ = bf16[128,4096]{1,0:T(8,128)(2,1)} fusion(bf16[32,4096]{1,0:T(8,128)(2,1)} %collective-permute-done.9, bf16[32,4096]{1,0:T(8,128)(2,1)} %collective-permute-done.8, bf16[32,4096]{1,0:T(8,128)(2,1)} %collective-permute-done.7, bf16[32,4096]{1,0:T(8,128)(2,1)S(1)} %maximum_select_fusion.6), kind=kLoop, calls=%fused_computation.32 | loop fusion | flops 4194304 | bytes 2097152 | tf_op jit(solution)/shard_map/concatenate | solution.py:169
  42.5 4.3 %collective-permute-start.10 = (bf16[128,4096]{1,0:T(8,128)(2,1)}, bf16[128,4096]{1,0:T(8,128)(2,1)S(1)}, u32[]{:S(2)}, u32[]{:S(2)}) collective-permute-start(bf16[128,4096]{1,0:T(8,128)(2,1)} %pad_maximum_fusion.1.refs_0_), channel_id=1, source_target_pairs={{0,48},{1,49},{2,50},{3,51},{4,52},{5,53},{6,54},{7,55},{8,56},{9,... | collective-permute-start | bytes 3145736 | tf_op jit(solution)/shard_map/ppermute | solution.py:59
  47.9 7.7 %collective-permute-done.15 = bf16[128,2048]{1,0:T(8,128)(2,1)} collective-permute-done((bf16[128,2048]{1,0:T(8,128)(2,1)}, bf16[128,2048]{1,0:T(8,128)(2,1)}, u32[]{:S(2)}, u32[]{:S(2)}) %collective-permute-start.15) | collective-permute-done | bytes 524320 | tf_op jit(solution)/shard_map/ppermute | solution.py:182
  63.1 2.2 %fusion.146 = f32[128,256]{1,0:T(8,128)S(1)} fusion(bf16[128,4096]{1,0:T(8,128)(2,1)} %collective-permute-done.12.refs_3_, bf16[4096,256]{1,0:T(8,128)(2,1)S(1)} %constant_dynamic-update-slice_fusion), kind=kOutput, calls=%fused_computation.234 | convolution fusion | flops 268435456 | bytes 3276800 | tf_op jit(solution)/shard_map/dot_general | solution.py:31
  69.7 2.3 %collective-permute-start.19 = (bf16[64,4096]{1,0:T(8,128)(2,1)S(1)}, bf16[64,4096]{1,0:T(8,128)(2,1)S(1)}, u32[]{:S(2)}, u32[]{:S(2)}) collective-permute-start(bf16[64,4096]{1,0:T(8,128)(2,1)S(1)} %slice.72), channel_id=1, source_target_pairs={{0,48},{1,49},{2,50},{3,51},{4,52},{5,53},{6,54},{7,55},{8,56},{9,... | collective-permute-start | bytes 1572872 | tf_op jit(solution)/shard_map/ppermute | solution.py:59
  77.2 2.3 %collective-permute-start.17 = (bf16[128,2048]{1,0:T(8,128)(2,1)}, bf16[128,2048]{1,0:T(8,128)(2,1)}, u32[]{:S(2)}, u32[]{:S(2)}) collective-permute-start(bf16[128,2048]{1,0:T(8,128)(2,1)} %get-tuple-element.21), channel_id=1, source_target_pairs={{0,16},{1,17},{2,18},{3,19},{4,20},{5,21},{6,22},{7,23},{8,24},{9,... | collective-permute-start | bytes 1572872 | tf_op jit(solution)/shard_map/ppermute | solution.py:59
  79.6 2.3 %collective-permute-start.18 = (bf16[128,2048]{1,0:T(8,128)(2,1)}, bf16[128,2048]{1,0:T(8,128)(2,1)}, u32[]{:S(2)}, u32[]{:S(2)}) collective-permute-start(bf16[128,2048]{1,0:T(8,128)(2,1)} %get-tuple-element.22), channel_id=1, source_target_pairs={{0,48},{1,49},{2,50},{3,51},{4,52},{5,53},{6,54},{7,55},{8,56},{9,... | collective-permute-start | bytes 1572872 | tf_op jit(solution)/shard_map/ppermute | solution.py:59
  86.6 2.4 %collective-permute-start.21 = (bf16[128,256]{1,0:T(8,128)(2,1)S(1)}, bf16[128,256]{1,0:T(8,128)(2,1)S(1)}, u32[]{:S(2)}, u32[]{:S(2)}) collective-permute-start(bf16[128,256]{1,0:T(8,128)(2,1)S(1)} %get-tuple-element.37), channel_id=1, source_target_pairs={{0,1},{1,0},{2,3},{3,2},{4,5},{5,4},{6,7},{7,6},{8,9},{9,8},{10,11... | collective-permute-start | bytes 196616 | tf_op jit(solution)/shard_map/ppermute | solution.py:209
  89.7 3.8 %collective-permute-done.21 = bf16[128,256]{1,0:T(8,128)(2,1)S(1)} collective-permute-done((bf16[128,256]{1,0:T(8,128)(2,1)S(1)}, bf16[128,256]{1,0:T(8,128)(2,1)S(1)}, u32[]{:S(2)}, u32[]{:S(2)}) %collective-permute-start.21) | collective-permute-done | bytes 65568 | tf_op jit(solution)/shard_map/ppermute | solution.py:209
  93.6 2.3 %convolution_convert_fusion.1 = bf16[128,2048]{1,0:T(8,128)(2,1)} fusion(bf16[128,256]{1,0:T(8,128)(2,1)S(1)} %collective-permute-done.21, bf16[128,256]{1,0:T(8,128)(2,1)S(1)} %get-tuple-element.37, bf16[128,2048]{1,0:T(8,128)(2,1)S(1)} %collective-permute-done.16, bf16[128,2048]{1,0:T(8,128)(2,1)} %collective-permute-done.15, ...), kind=kOutput, calls=%fused_computation.13 | convolution fusion | flops 279445504 | bytes 2752512 | tf_op jit(solution)/shard_map/dot_general | solution.py:31
  99.8 8.3 %collective-permute-done.22 = bf16[128,2048]{1,0:T(8,128)(2,1)} collective-permute-done((bf16[128,2048]{1,0:T(8,128)(2,1)}, bf16[128,2048]{1,0:T(8,128)(2,1)}, u32[]{:S(2)}, u32[]{:S(2)}) %collective-permute-start.22) | collective-permute-done | bytes 524320 | tf_op jit(solution)/shard_map/ppermute | solution.py:59
  108.0 2.7 %fusion.144 = (bf16[128,2048]{1,0:T(8,128)(2,1)S(1)}, f32[128,2048]{1,0:T(8,128)S(1)}) fusion(bf16[128,2048]{1,0:T(8,128)(2,1)} %collective-permute-done.22, bf16[128,2048]{1,0:T(8,128)(2,1)} %collective-permute-done.18, bf16[128,2048]{1,0:T(8,128)(2,1)} %collective-permute-done.17, bf16[128,2048]{1,0:T(8,128)(2,1)} %copy-done.19, ...), kind=kOutput, calls=%fused_computation.232 | convolution fusion | flops 281018368 | bytes 5636096 | tf_op jit(solution)/shard_map/dot_general | solution.py:31
  112.4 2.1 %collective-permute-start.24 = (bf16[32,2048]{1,0:T(8,128)(2,1)S(1)}, bf16[32,2048]{1,0:T(8,128)(2,1)S(1)}, u32[]{:S(2)}, u32[]{:S(2)}) collective-permute-start(bf16[32,2048]{1,0:T(8,128)(2,1)S(1)} %get-tuple-element.34), channel_id=1, source_target_pairs={{0,8},{1,9},{2,10},{3,11},{4,12},{5,13},{6,14},{7,15},{8,0},{9,1},... | collective-permute-start | bytes 393224 | tf_op jit(solution)/shard_map/ppermute | solution.py:59
  119.6 3.8 %convolution_add_fusion = f32[256,2048]{1,0:T(8,128)} fusion(f32[256,2048]{1,0:T(8,128)} %collective-permute-done.5, bf16[256,512]{1,0:T(8,128)(2,1)S(1)} %copy-done.14, bf16[512,4096]{1,0:T(8,128)(2,1)S(1)} %copy-done.6, s32[]{:T(128)S(6)} %select_n.334), kind=kOutput, calls=%fused_computation.8 | convolution fusion | flops 537395200 | bytes 6553604 | tf_op jit(solution)/shard_map/dot_general | solution.py:31
  123.4 4.4 %fusion = f32[1024,128]{1,0:T(8,128)} fusion(bf16[2048,2048]{1,0:T(8,128)(2,1)} %all-gather.2.cloned.1.call-done, bf16[128,4096]{1,0:T(8,128)(2,1)} %param.13), kind=kOutput, calls=%fused_computation.2 | convolution fusion | flops 536870912 | bytes 5242880 | tf_op jit(solution)/shard_map/dot_general | solution.py:35
  127.7 6.5 %fusion.27.refs_8_ = bf16[1024,128]{1,0:T(8,128)(2,1)} fusion(s32[1024]{0:T(1024)S(1)} %eq.73, f32[1024,128]{1,0:T(8,128)} %fusion, bf16[2048,2048]{1,0:T(8,128)(2,1)} %all-gather.2.cloned.1.call-done, f32[1024,128]{1,0:T(8,128)} %bitcast.36, f32[1024,128]{1,0:T(8,128)} %get-tuple-element.29, f32[1024,128]{1,0:T(8,128)} %get-tuple-element.28, ...), kind=kOutput, calls=%fused_computation.30 | convolution fusion | flops 808321024 | bytes 7081984 | tf_op jit(solution)/shard_map/dot_general | solution.py:31
  134.2 8.0 %shard_map.112 = bf16[128,4096]{1,0:T(8,128)(2,1)} custom-call(bf16[1024,128]{1,0:T(8,128)(2,1)} %get-tuple-element.27.hidden_ref, bf16[2,1024,2048]{2,1,0:T(8,128)(2,1)} %bitcast.35), custom_call_target="tpu_custom_call" | custom-call | flops 1073741824 | bytes 9437184 | tf_op jit(solution)/shard_map/pallas_call | solution.py:84
  148.4 8.4 %shard_map.113 = bf16[4096,128]{1,0:T(8,128)(2,1)} custom-call(bf16[128,4096]{1,0:T(8,128)(2,1)} %pad_maximum_fusion.1.refs_0_, bf16[128,4096]{1,0:T(8,128)(2,1)} %copy-done.3, bf16[128,4096]{1,0:T(8,128)(2,1)} %constant_dynamic-update-slice_fusion.2.refs_2_, bf16[128,4096]{1,0:T(8,128)(2,1)} %collective-permute-done.12.refs_3_, ...), custom_call_target="tpu_custom_call" | custom-call | flops 1073741824 | bytes 9437184 | tf_op jit(solution)/shard_map/pallas_call | solution.py:110
  156.7 5.3 %collective-permute-done.6 = bf16[256,1024]{1,0:T(8,128)(2,1)} collective-permute-done((bf16[256,1024]{1,0:T(8,128)(2,1)}, bf16[256,1024]{1,0:T(8,128)(2,1)}, u32[]{:S(2)}, u32[]{:S(2)}) %collective-permute-start.6) | collective-permute-done | bytes 524320 | tf_op jit(solution)/shard_map/ppermute | solution.py:213
  162.0 2.8 %add_convert_fusion = bf16[256,1024]{1,0:T(8,128)(2,1)} fusion(bf16[256,1024]{1,0:T(8,128)(2,1)} %collective-permute-done.6, f32[256,2048]{1,0:T(8,128)} %convolution_add_fusion, s32[]{:T(128)S(6)} %select_n.336, f32[16,1024]{1,0:T(8,128)S(1)} %collective-permute-done.28, f32[16,1024]{1,0:T(8,128)S(1)} %get-tuple-element.35, ...), kind=kOutput, calls=%fused_computation.33 | convolution fusion | flops 101851136 | bytes 2228485 | tf_op jit(solution)/shard_map/dot_general | solution.py:272
  (145 shorter events, 59.3 us)
Async XLA Ops:
  7.2 116.2 %all-gather.2.cloned.1.call-start = ((), (), s32[]{:S(2)}) async-start(), calls=%async_computation | async-start | bytes 8454144 | tf_op jit(solution)/shard_map/all_gather | solution.py:156
  22.2 10.1 %collective-permute-start.7 = (bf16[32,4096]{1,0:T(8,128)(2,1)S(1)}, bf16[32,4096]{1,0:T(8,128)(2,1)}, u32[]{:S(2)}, u32[]{:S(2)}) collective-permute-start(bf16[32,4096]{1,0:T(8,128)(2,1)S(1)} %maximum_select_fusion.6), channel_id=1, source_target_pairs={{0,12},{1,13},{2,14},{3,15},{4,0},{5,1},{6,2},{7,3},{8,4},{9,5},{1... | collective-permute-start | bytes 786440 | tf_op jit(solution)/shard_map/ppermute | solution.py:59
  25.3 8.2 %collective-permute-start.8 = (bf16[32,4096]{1,0:T(8,128)(2,1)S(1)}, bf16[32,4096]{1,0:T(8,128)(2,1)}, u32[]{:S(2)}, u32[]{:S(2)}) collective-permute-start(bf16[32,4096]{1,0:T(8,128)(2,1)S(1)} %maximum_select_fusion.6), channel_id=1, source_target_pairs={{0,8},{1,9},{2,10},{3,11},{4,12},{5,13},{6,14},{7,15},{8,0},{9,1},... | collective-permute-start | bytes 786440 | tf_op jit(solution)/shard_map/ppermute | solution.py:59
  26.0 10.5 %collective-permute-start.9 = (bf16[32,4096]{1,0:T(8,128)(2,1)S(1)}, bf16[32,4096]{1,0:T(8,128)(2,1)}, u32[]{:S(2)}, u32[]{:S(2)}) collective-permute-start(bf16[32,4096]{1,0:T(8,128)(2,1)S(1)} %maximum_select_fusion.6), channel_id=1, source_target_pairs={{0,4},{1,5},{2,6},{3,7},{4,8},{5,9},{6,10},{7,11},{8,12},{9,13},{1... | collective-permute-start | bytes 786440 | tf_op jit(solution)/shard_map/ppermute | solution.py:59
  26.9 28.7 %collective-permute-start.11 = (bf16[4096,128]{1,0:T(8,128)(2,1)}, bf16[4096,128]{1,0:T(8,128)(2,1)}, u32[]{:S(2)}, u32[]{:S(2)}) collective-permute-start(bf16[4096,128]{1,0:T(8,128)(2,1)} %param.12), channel_id=1, source_target_pairs={{0,64},{64,0},{1,65},{65,1},{2,66},{66,2},{3,67},{67,3},{4,68},{68... | collective-permute-start | bytes 3145736 | tf_op jit(solution)/shard_map/ppermute | solution.py:178
  27.8 20.0 %collective-permute-start.3 = (bf16[128,2048]{1,0:T(8,128)(2,1)}, bf16[128,2048]{1,0:T(8,128)(2,1)}, u32[]{:S(2)}, u32[]{:S(2)}) collective-permute-start(bf16[128,2048]{1,0:T(8,128)(2,1)} %constant_dynamic-slice_fusion.6), channel_id=1, source_target_pairs={{0,1},{1,0},{2,3},{3,2},{4,5},{5,4},{6,7},{7,6},{8,9},{9,8},{10,11... | collective-permute-start | bytes 1572872 | tf_op jit(solution)/shard_map/ppermute | solution.py:188
  40.3 15.3 %collective-permute-start.15 = (bf16[128,2048]{1,0:T(8,128)(2,1)}, bf16[128,2048]{1,0:T(8,128)(2,1)}, u32[]{:S(2)}, u32[]{:S(2)}) collective-permute-start(bf16[128,2048]{1,0:T(8,128)(2,1)} %pad_maximum_fusion.3), channel_id=1, source_target_pairs={{0,1},{1,0},{2,3},{3,2},{4,5},{5,4},{6,7},{7,6},{8,9},{9,8},{10,11... | collective-permute-start | bytes 1572872 | tf_op jit(solution)/shard_map/ppermute | solution.py:182
  42.5 19.4 %collective-permute-start.10 = (bf16[128,4096]{1,0:T(8,128)(2,1)}, bf16[128,4096]{1,0:T(8,128)(2,1)S(1)}, u32[]{:S(2)}, u32[]{:S(2)}) collective-permute-start(bf16[128,4096]{1,0:T(8,128)(2,1)} %pad_maximum_fusion.1.refs_0_), channel_id=1, source_target_pairs={{0,48},{1,49},{2,50},{3,51},{4,52},{5,53},{6,54},{7,55},{8,56},{9,... | collective-permute-start | bytes 3145736 | tf_op jit(solution)/shard_map/ppermute | solution.py:59
  46.8 16.3 %collective-permute-start.12 = (bf16[128,4096]{1,0:T(8,128)(2,1)}, bf16[128,4096]{1,0:T(8,128)(2,1)}, u32[]{:S(2)}, u32[]{:S(2)}) collective-permute-start(bf16[128,4096]{1,0:T(8,128)(2,1)} %pad_maximum_fusion.1.refs_0_), channel_id=1, source_target_pairs={{0,16},{1,17},{2,18},{3,19},{4,20},{5,21},{6,22},{7,23},{8,24},{9,... | collective-permute-start | bytes 3145736 | tf_op jit(solution)/shard_map/ppermute | solution.py:59
  47.8 25.4 %collective-permute-start.14 = (bf16[128,2048]{1,0:T(8,128)(2,1)S(1)}, bf16[128,2048]{1,0:T(8,128)(2,1)S(1)}, u32[]{:S(2)}, u32[]{:S(2)}) collective-permute-start(bf16[128,2048]{1,0:T(8,128)(2,1)S(1)} %pad_maximum_fusion.2), channel_id=1, source_target_pairs={{0,64},{64,0},{1,65},{65,1},{2,66},{66,2},{3,67},{67,3},{4,68},{68... | collective-permute-start | bytes 1572872 | tf_op jit(solution)/shard_map/ppermute | solution.py:183
  55.6 17.7 %collective-permute-start.16 = (bf16[128,2048]{1,0:T(8,128)(2,1)}, bf16[128,2048]{1,0:T(8,128)(2,1)S(1)}, u32[]{:S(2)}, u32[]{:S(2)}) collective-permute-start(bf16[128,2048]{1,0:T(8,128)(2,1)} %collective-permute-done.15), channel_id=1, source_target_pairs={{0,64},{64,0},{1,65},{65,1},{2,66},{66,2},{3,67},{67,3},{4,68},{68... | collective-permute-start | bytes 1572872 | tf_op jit(solution)/shard_map/ppermute | solution.py:184
  65.5 8.8 %collective-permute-start.13 = (bf16[384,256]{1,0:T(8,128)(2,1)S(1)}, bf16[384,256]{1,0:T(8,128)(2,1)S(1)}, u32[]{:S(2)}, u32[]{:S(2)}) collective-permute-start(bf16[384,256]{1,0:T(8,128)(2,1)S(1)} %fusion.63), channel_id=1, source_target_pairs={{0,1},{1,0},{2,3},{3,2},{4,5},{5,4},{6,7},{7,6},{8,9},{9,8},{10,11... | collective-permute-start | bytes 589832 | tf_op jit(solution)/shard_map/ppermute | solution.py:207
  69.7 49.8 %collective-permute-start.5 = (f32[256,2048]{1,0:T(8,128)}, f32[256,2048]{1,0:T(8,128)}, u32[]{:S(2)}, u32[]{:S(2)}) collective-permute-start(f32[256,2048]{1,0:T(8,128)} %fusion.14), channel_id=1, source_target_pairs={{0,64},{64,0},{1,65},{65,1},{2,66},{66,2},{3,67},{67,3},{4,68},{68... | collective-permute-start | bytes 6291464 | tf_op jit(solution)/shard_map/ppermute | solution.py:194
  69.7 12.1 %collective-permute-start.19 = (bf16[64,4096]{1,0:T(8,128)(2,1)S(1)}, bf16[64,4096]{1,0:T(8,128)(2,1)S(1)}, u32[]{:S(2)}, u32[]{:S(2)}) collective-permute-start(bf16[64,4096]{1,0:T(8,128)(2,1)S(1)} %slice.72), channel_id=1, source_target_pairs={{0,48},{1,49},{2,50},{3,51},{4,52},{5,53},{6,54},{7,55},{8,56},{9,... | collective-permute-start | bytes 1572872 | tf_op jit(solution)/shard_map/ppermute | solution.py:59
  73.2 10.6 %collective-permute-start.20 = (bf16[64,4096]{1,0:T(8,128)(2,1)S(1)}, bf16[64,4096]{1,0:T(8,128)(2,1)S(1)}, u32[]{:S(2)}, u32[]{:S(2)}) collective-permute-start(bf16[64,4096]{1,0:T(8,128)(2,1)S(1)} %slice.73), channel_id=1, source_target_pairs={{0,16},{1,17},{2,18},{3,19},{4,20},{5,21},{6,22},{7,23},{8,24},{9,... | collective-permute-start | bytes 1572872 | tf_op jit(solution)/shard_map/ppermute | solution.py:59
  77.2 22.5 %collective-permute-start.17 = (bf16[128,2048]{1,0:T(8,128)(2,1)}, bf16[128,2048]{1,0:T(8,128)(2,1)}, u32[]{:S(2)}, u32[]{:S(2)}) collective-permute-start(bf16[128,2048]{1,0:T(8,128)(2,1)} %get-tuple-element.21), channel_id=1, source_target_pairs={{0,16},{1,17},{2,18},{3,19},{4,20},{5,21},{6,22},{7,23},{8,24},{9,... | collective-permute-start | bytes 1572872 | tf_op jit(solution)/shard_map/ppermute | solution.py:59
  79.6 20.2 %collective-permute-start.18 = (bf16[128,2048]{1,0:T(8,128)(2,1)}, bf16[128,2048]{1,0:T(8,128)(2,1)}, u32[]{:S(2)}, u32[]{:S(2)}) collective-permute-start(bf16[128,2048]{1,0:T(8,128)(2,1)} %get-tuple-element.22), channel_id=1, source_target_pairs={{0,48},{1,49},{2,50},{3,51},{4,52},{5,53},{6,54},{7,55},{8,56},{9,... | collective-permute-start | bytes 1572872 | tf_op jit(solution)/shard_map/ppermute | solution.py:59
  95.9 12.1 %collective-permute-start.22 = (bf16[128,2048]{1,0:T(8,128)(2,1)}, bf16[128,2048]{1,0:T(8,128)(2,1)}, u32[]{:S(2)}, u32[]{:S(2)}) collective-permute-start(bf16[128,2048]{1,0:T(8,128)(2,1)} %convolution_convert_fusion.1), channel_id=1, source_target_pairs={{0,32},{1,33},{2,34},{3,35},{4,36},{5,37},{6,38},{7,39},{8,40},{9,... | collective-permute-start | bytes 1572872 | tf_op jit(solution)/shard_map/ppermute | solution.py:59
  99.5 48.7 %collective-permute-start.29 = (bf16[128,4096]{1,0:T(8,128)(2,1)S(1)}, bf16[128,4096]{1,0:T(8,128)(2,1)}, u32[]{:S(2)}, u32[]{:S(2)}) collective-permute-start(bf16[128,4096]{1,0:T(8,128)(2,1)S(1)} %copy-done.2), channel_id=1, source_target_pairs={{0,64},{64,0},{1,65},{65,1},{2,66},{66,2},{3,67},{67,3},{4,68},{68... | collective-permute-start | bytes 3145736 | tf_op jit(solution)/shard_map/ppermute | solution.py:267
  117.0 31.3 %collective-permute-start.30 = (bf16[128,4096]{1,0:T(8,128)(2,1)S(1)}, bf16[128,4096]{1,0:T(8,128)(2,1)}, u32[]{:S(2)}, u32[]{:S(2)}) collective-permute-start(bf16[128,4096]{1,0:T(8,128)(2,1)S(1)} %copy-done.4), channel_id=1, source_target_pairs={{0,64},{64,0},{1,65},{65,1},{2,66},{66,2},{3,67},{67,3},{4,68},{68... | collective-permute-start | bytes 3145736 | tf_op jit(solution)/shard_map/ppermute | solution.py:267
  118.8 29.5 %collective-permute-start.32 = (bf16[128,4096]{1,0:T(8,128)(2,1)}, bf16[128,4096]{1,0:T(8,128)(2,1)}, u32[]{:S(2)}, u32[]{:S(2)}) collective-permute-start(bf16[128,4096]{1,0:T(8,128)(2,1)} %collective-permute-done.12.refs_3_), channel_id=1, source_target_pairs={{0,64},{64,0},{1,65},{65,1},{2,66},{66,2},{3,67},{67,3},{4,68},{68... | collective-permute-start | bytes 3145736 | tf_op jit(solution)/shard_map/ppermute | solution.py:267
  119.5 28.9 %collective-permute-start.31 = (bf16[128,4096]{1,0:T(8,128)(2,1)}, bf16[128,4096]{1,0:T(8,128)(2,1)}, u32[]{:S(2)}, u32[]{:S(2)}) collective-permute-start(bf16[128,4096]{1,0:T(8,128)(2,1)} %constant_dynamic-update-slice_fusion.2.refs_2_), channel_id=1, source_target_pairs={{0,64},{64,0},{1,65},{65,1},{2,66},{66,2},{3,67},{67,3},{4,68},{68... | collective-permute-start | bytes 3145736 | tf_op jit(solution)/shard_map/ppermute | solution.py:267
  146.7 15.3 %collective-permute-start.6 = (bf16[256,1024]{1,0:T(8,128)(2,1)}, bf16[256,1024]{1,0:T(8,128)(2,1)}, u32[]{:S(2)}, u32[]{:S(2)}) collective-permute-start(bf16[256,1024]{1,0:T(8,128)(2,1)} %dynamic-slice_convert_fusion), channel_id=1, source_target_pairs={{0,1},{1,0},{2,3},{3,2},{4,5},{5,4},{6,7},{7,6},{8,9},{9,8},{10,11... | collective-permute-start | bytes 1572872 | tf_op jit(solution)/shard_map/ppermute | solution.py:213
  148.2 13.8 %collective-permute-start.28 = (f32[16,1024]{1,0:T(8,128)S(1)}, f32[16,1024]{1,0:T(8,128)S(1)}, u32[]{:S(2)}, u32[]{:S(2)}) collective-permute-start(f32[16,1024]{1,0:T(8,128)S(1)} %get-tuple-element.36), channel_id=1, source_target_pairs={{0,64},{64,0},{1,65},{65,1},{2,66},{66,2},{3,67},{67,3},{4,68},{68... | collective-permute-start | bytes 196616 | tf_op jit(solution)/shard_map/ppermute | solution.py:269
  (31 other events, 268.6 us)
Sparse Core Ops, SparseCore 0:
  13.0 95.8 all-gather.1
where the time goes:
time: 173 us; the launch traced here: 172 us
  waiting for transfers between devices  47 us (27%)
  starting transfers between devices  35 us (20%)
  matrix products  33.6 us (19%)
  Pallas kernels  16.3 us (9%)
  local copies, waits for them, and re-layouts  15.7 us (9%)
  between operations  15.2 us (9%)
  other arithmetic  8.74 us (5%)
    ppermute x16, starting transfers between devices, moved(): lax.ppermute(x, axes, [(number(p), number(step(*p))) for p in places])  26.3 us
    dot_general x11, matrix products, dot(): return jnp.dot(left, right, preferred_element_type=jnp.float32)  25.8 us
    ppermute x16, waiting for transfers between devices, moved(): lax.ppermute(x, axes, [(number(p), number(step(*p))) for p in places])  25.5 us
    pallas_call x1, Pallas kernels, grad_in_of(): pl.pallas_call(kernel, grid=(features // tile,), in_specs=[pl.BlockSpec((...  8.39 us
    pallas_call x1, Pallas kernels, grad_out_of(): pl.pallas_call(kernel, grid=(sides * per_side,), in_specs=[pl.BlockSpec((...  7.96 us
    ppermute x1, waiting for transfers between devices, per_device(): got_out = lax.ppermute(given, 'xh', swap)  7.7 us
    ppermute x1, waiting for transfers between devices, per_device(): light_got = lax.ppermute(light_given, 'xh', swap)  5.28 us
    dot_general x1, matrix products, general(): lax.dot_general(left, right, ((left_dims, right_dims), ((), ())), preferr...  4.35 us
  transfers between devices with their start and end apart: 34, of which 18 were waited for; matrix products, arithmetic and copies ran while one was open for 29% of the time, Pallas kernels for 10%

commit v1 on v0

--- a/solution.py
+++ b/solution.py
@@ -4,6 +4,7 @@
 import jax.numpy as jnp
 from jax import lax
 from jax.experimental import pallas as pl
+from jax.experimental.pallas import tpu as pltpu
 from jax.sharding import Mesh, PartitionSpec as P
 
 
@@ -67,51 +68,76 @@
     return lambda b, z, y, xl, xh: (b, z + by * (1 - b), y + by * b, xl, xh)
 
 
-def rows_product(left, tiles):
-    return lax.dot_general(
-        left, tiles, (((0,), (0,)), ((), ())), preferred_element_type=jnp.float32
-    )
-
-
-def grad_out_of(hidden, back, tile=512):
-    sides, rows, width = back.shape
-    units = hidden.shape[1]
-    per_side = width // tile
-
-    def kernel(hidden_ref, back_ref, out_ref):
-        out_ref[...] = rows_product(hidden_ref[...], back_ref[0]).astype(out_ref.dtype)
+def grad_out_of(pre, weight, back, places, tile=512):
+    rows, features = back.shape
+    units = pre.shape[1]
+    last = features // tile - 1
+
+    def kernel(pre_ref, weight_ref, back_ref, places_ref, out_ref, slope_ref, hidden, total):
+        step = pl.program_id(0)
+
+        @pl.when(step == 0)
+        def _():
+            hidden[...] = gelu_tanh(pre_ref[...]).T.astype(hidden.dtype)
+            total[...] = jnp.zeros_like(total)
+
+        tiles = back_ref[...]
+        out_ref[...] = dot(hidden[...], tiles).astype(out_ref.dtype)
+        total[...] += general(tiles, weight_ref[...], (1,), (1,))
+
+        @pl.when(step == last)
+        def _():
+            slope = (total[...] * gelu_slope(pre_ref[...])).T.astype(slope_ref.dtype)
+            for at in range(0, rows, 256):
+                target = at + lax.broadcasted_iota(jnp.int32, (256, rows), 0)
+                moves = (target == places_ref[...]).astype(jnp.float32).astype(slope.dtype)
+                slope_ref[:, at : at + 256] = general(slope, moves, (1,), (1,)).astype(
+                    slope_ref.dtype
+                )
 
     return pl.pallas_call(
         kernel,
-        grid=(sides * per_side,),
+        grid=(last + 1,),
         in_specs=[
             pl.BlockSpec((rows, units), lambda i: (0, 0)),
-            pl.BlockSpec((1, rows, tile), lambda i: (i // per_side, 0, i % per_side)),
+            pl.BlockSpec((units, tile), lambda i: (0, i)),
+            pl.BlockSpec((rows, tile), lambda i: (0, i)),
+            pl.BlockSpec((1, rows), lambda i: (0, 0)),
         ],
-        out_specs=pl.BlockSpec((units, tile), lambda i: (0, i)),
-        out_shape=jax.ShapeDtypeStruct((units, sides * width), jnp.bfloat16),
+        out_specs=[
+            pl.BlockSpec((units, tile), lambda i: (0, i)),
+            pl.BlockSpec((units, rows), lambda i: (0, 0)),
+        ],
+        out_shape=[
+            jax.ShapeDtypeStruct((units, features), jnp.bfloat16),
+            jax.ShapeDtypeStruct((units, rows), jnp.bfloat16),
+        ],
+        scratch_shapes=[
+            pltpu.VMEM((units, rows), jnp.bfloat16),
+            pltpu.VMEM((rows, units), jnp.float32),
+        ],
         cost_estimate=pl.CostEstimate(
-            flops=2 * rows * units * sides * width,
-            bytes_accessed=2 * (sides * rows * width + units * sides * width),
+            flops=4 * rows * units * features,
+            bytes_accessed=2 * (rows * features + 2 * units * features),
             transcendentals=0,
         ),
-    )(hidden, back)
+    )(pre, weight, back, places)
 
 
 def grad_in_of(sheets, slope, tile=512):
     tall, features = sheets[0].shape
-    rows, units = slope.shape
+    units, rows = slope.shape
 
     def kernel(*refs):
         slope_ref, out_ref = refs[-2:]
         tiles = jnp.concatenate([ref[...] for ref in refs[:-2]], axis=0)
-        out_ref[...] = rows_product(slope_ref[...], tiles).T.astype(out_ref.dtype)
+        out_ref[...] = dot(slope_ref[...], tiles).T.astype(out_ref.dtype)
 
     return pl.pallas_call(
         kernel,
         grid=(features // tile,),
         in_specs=[pl.BlockSpec((tall, tile), lambda i: (0, i)) for _ in sheets]
-        + [pl.BlockSpec((rows, units), lambda i: (0, 0))],
+        + [pl.BlockSpec((units, rows), lambda i: (0, 0))],
         out_specs=pl.BlockSpec((tile, units), lambda i: (i, 0)),
         out_shape=jax.ShapeDtypeStruct((features, units), jnp.bfloat16),
         cost_estimate=pl.CostEstimate(
@@ -149,25 +175,22 @@
     row_scale = jnp.where(live_slots, route_gate[0], jnp.zeros_like(route_gate[0]))
     own_positions = part(positions, core, half, 0)
     own_scale = part(row_scale, core, half, 0)
-    picked = jnp.take(tokens, own_positions, axis=0, mode="clip")
-    picked, later_positions = lax.optimization_barrier((picked, own_positions))
-    back = jnp.take(cotangent, later_positions, axis=0, mode="clip").astype(jnp.float32)
+    back = jnp.take(cotangent, own_positions, axis=0, mode="clip").astype(jnp.float32)
     back = (back * own_scale[:, None]).astype(jnp.bfloat16)
-    back = lax.all_gather(back, ("xh", "xl", "y", "z", "b"), axis=0, tiled=True)
-    back = back.reshape(2, back.shape[0] // 2, width)
-
-    over_side = moved(picked, lambda b, z, y, xl, xh: (b, z, y, xl, xh + 1))
-    over_low = moved(picked, lambda b, z, y, xl, xh: (b, z, y, xl + 1, xh))
-    over_both = moved(picked, lambda b, z, y, xl, xh: (b, z, y, xl + 1, xh + 1))
-    plane = ordered(
-        low == 0,
-        ordered(side == 0, picked, over_side, 1),
-        ordered(side == 0, over_low, over_both, 1),
-        0,
-    )
-    plane, later_tokens = lax.optimization_barrier((plane, tokens))
-    sheet = jnp.concatenate([plane] + [moved(plane, second(-k)) for k in (1, 2, 3)], axis=0)
-    sheet, later_out = lax.optimization_barrier((sheet, heavy_out))
+    both = jnp.concatenate([jnp.take(tokens, own_positions, axis=0, mode="clip"), back], axis=0)
+
+    over_side = moved(both, lambda b, z, y, xl, xh: (b, z, y, xl, xh + 1))
+    over_low = moved(both, lambda b, z, y, xl, xh: (b, z, y, xl + 1, xh))
+    over_both = moved(both, lambda b, z, y, xl, xh: (b, z, y, xl + 1, xh + 1))
+
+    mine = ordered(side == 0, both, over_side, 1)
+    other = ordered(side == 0, over_low, over_both, 1)
+    plane = ordered(low == 0, mine[:half], other[:half], 0)
+    back = ordered(low == 0, mine[half:], other[half:], 0)
+    back = lax.all_gather(back, ("z", "y", "b"), axis=0, tiled=True)
+    plane, later_tokens, later_out = lax.optimization_barrier((plane, tokens, heavy_out))
+    sheet = [plane] + [moved(plane, second(-k)) for k in (1, 2, 3)]
+    sheet = jnp.concatenate(sheet, axis=0)
     after = moved(sheet, third(-1))
     before = moved(sheet, third(1))
     cut = sheet.shape[0] // 2
@@ -226,13 +249,10 @@
         total = total + one.astype(jnp.float32)
     count = 4 * tall
     r = jnp.arange(count, dtype=jnp.int32)
-    r_slot, r_z, r_y, r_low = r % half, r // half % 4, r // (4 * half) % 4, r // (16 * half)
+    inner, r_y, r_z = r % strip, r // strip % 4, r // tall
     turn_z, turn_y = (r_z - at_z) % 4, (r_y - at_y) % 4
-    inner = r_low * half + r_slot
-    place = jnp.where(core == 0, turn_z * 4 + turn_y, turn_y * 4 + turn_z) * (2 * half) + inner
-    place_other = (
-        jnp.where(core == 0, turn_y * 4 + turn_z, turn_z * 4 + turn_y) * (2 * half) + inner
-    )
+    place = jnp.where(core == 0, turn_z * 4 + turn_y, turn_y * 4 + turn_z) * strip + inner
+    place_other = jnp.where(core == 0, turn_y * 4 + turn_z, turn_z * 4 + turn_y) * strip + inner
     choice = (place[:, None] == r[None, :]).astype(jnp.bfloat16)
 
     pre_act = jnp.concatenate(pre_acts, axis=0)
@@ -244,22 +264,17 @@
     )
 
     def both_cores(own, theirs):
-        pieces = [own.reshape(-1, 1, half, units), theirs.reshape(-1, 1, half, units)]
+        pieces = [own.reshape(-1, 1, strip, units), theirs.reshape(-1, 1, strip, units)]
         return ordered(core == 0, pieces[0], pieces[1], 1).reshape(2 * count, units)
 
     pre_all = both_cores(pre_rows[:, :units], lax.ppermute(pre_rows[:, units:], "b", swap))
-    hidden_all = gelu_tanh(pre_all).astype(jnp.bfloat16)
-    slope = general(back[0], heavy_out[:, :width], (1,), (1,)) + general(
-        back[1], heavy_out[:, width:], (1,), (1,)
-    )
-    slope = (slope * gelu_slope(pre_all)).astype(jnp.bfloat16)
-    grad_out = grad_out_of(hidden_all, back)
-    places = jnp.stack([place, place_other + count])
-    places = jnp.where(core == 0, places, places[::-1])
-    places = places.reshape(2, -1, half).swapaxes(0, 1).reshape(-1)
-    wide = jnp.arange(2 * count, dtype=jnp.int32)
-    back_choice = (wide[:, None] == places[None, :]).astype(jnp.bfloat16)
-    slope_rows = dot(back_choice, slope).astype(jnp.bfloat16)
+    places = jnp.where(
+        core == 0,
+        jnp.stack([place, place_other + count]),
+        jnp.stack([place_other + count, place]),
+    )
+    places = places.reshape(2, -1, strip).swapaxes(0, 1).reshape(1, -1)
+    grad_out, slope_rows = grad_out_of(pre_all, heavy_out, back, places)
     total, slope_rows, grad_out = lax.optimization_barrier((total, slope_rows, grad_out))
     homed = part(total, low, half, 0) + lax.ppermute(
         part(total, 1 - low, half, 0).astype(jnp.bfloat16), "xl", swap

time: 173 us -> 165 us (0.954)
  matrix products: 33.6 us -> 19.6 us
  starting transfers between devices: 35 us -> 42.3 us
  waiting for transfers between devices: 47 us -> 50.7 us
  other arithmetic: 8.74 us -> 5.33 us
  local copies, waits for them, and re-layouts: 15.7 us -> 12.3 us
  Pallas kernels: 16.3 us -> 19.1 us
    dot_general x11 -> x10, matrix products: 25.8 us -> 16.1 us  [dot(): return jnp.dot(left, right, preferred_element_type=jnp.float32)]
    ppermute x1, waiting for transfers between devices: 0.01 us -> 8.66 us  [per_device(): got = lax.ppermute(sent, 'xh', swap)]
    ppermute x16, starting transfers between devices: 26.3 us -> 32.9 us  [moved(): lax.ppermute(x, axes, [(number(p), number(step(*p))) for p in places])]
    ppermute x1, waiting for transfers between devices: 7.7 us -> 1.67 us  [per_device(): got_out = lax.ppermute(given, 'xh', swap)]
    dot_general x1 -> x0, matrix products: 4.35 us -> none  [general(): lax.dot_general(left, right, ((left_dims, right_dims), ((), ())), preferr...]
    ppermute x16, waiting for transfers between devices: 25.5 us -> 29.8 us  [moved(): lax.ppermute(x, axes, [(number(p), number(step(*p))) for p in places])]
    ppermute x1, waiting for transfers between devices: 3.83 us -> 0.66 us  [per_device(): across = lax.ppermute(late, 'xh', swap)]
    pallas_call x1, Pallas kernels: 7.96 us -> 10.7 us  [grad_out_of(): pl.pallas_call(kernel, grid=(last + 1,), in_specs=[pl.BlockSpec((rows, un...]
  transfers between devices with their start and end apart: 34 -> 34, of which waited for: 18 -> 18; matrix products, arithmetic and copies ran while one was open for 29% -> 17% of each run, Pallas kernels for 10% -> 12%
where the time goes in v1:
time: 165 us; the launch traced here: 164 us
  waiting for transfers between devices  50.7 us (31%)
  starting transfers between devices  42.3 us (26%)
  matrix products  19.6 us (12%)
  Pallas kernels  19.1 us (12%)
  between operations  15.2 us (9%)
  local copies, waits for them, and re-layouts  12.3 us (7%)
  other arithmetic  5.33 us (3%)
    ppermute x16, starting transfers between devices, moved(): lax.ppermute(x, axes, [(number(p), number(step(*p))) for p in places])  32.9 us
    ppermute x16, waiting for transfers between devices, moved(): lax.ppermute(x, axes, [(number(p), number(step(*p))) for p in places])  29.8 us
    dot_general x10, matrix products, dot(): return jnp.dot(left, right, preferred_element_type=jnp.float32)  16.1 us
    pallas_call x1, Pallas kernels, grad_out_of(): pl.pallas_call(kernel, grid=(last + 1,), in_specs=[pl.BlockSpec((rows, un...  10.7 us
    ppermute x1, waiting for transfers between devices, per_device(): got = lax.ppermute(sent, 'xh', swap)  8.66 us
    pallas_call x1, Pallas kernels, grad_in_of(): pl.pallas_call(kernel, grid=(features // tile,), in_specs=[pl.BlockSpec((...  8.36 us
    ppermute x1, waiting for transfers between devices, per_device(): light_got = lax.ppermute(light_given, 'xh', swap)  4.54 us
    ppermute x1, waiting for transfers between devices, per_device(): early = jnp.concatenate([early, lax.ppermute(early, 'xh', swap)], axis=1)  3.69 us
  transfers between devices with their start and end apart: 34, of which 18 were waited for; matrix products, arithmetic and copies ran while one was open for 17% of the time, Pallas kernels for 12%

profile of v1, /device:TPU:0, one launch (start us, length us, event | category | flops | bytes accessed | tf_op | source)
XLA Modules:
  0.0 164.5 jit_solution(6827114293440362627)
XLA Ops:
  10.6 2.0 %gather_fusion = bf16[16,2048]{1,0:T(8,128)(2,1)S(1)} fusion(bf16[256,2048]{1,0:T(8,128)(2,1)} %param.9, s32[1024]{0:T(1024)S(1)} %pad_clamp_fusion), kind=kCustom, calls=%fused_computation | custom fusion | bytes 131136 | tf_op jit(solution)/shard_map/jit(_take)/gather | solution.py:180
  14.4 2.1 %collective-permute-start.2 = (bf16[32,2048]{1,0:T(8,128)(2,1)S(1)}, bf16[32,2048]{1,0:T(8,128)(2,1)S(1)}, u32[]{:S(2)}, u32[]{:S(2)}) collective-permute-start(bf16[32,2048]{1,0:T(8,128)(2,1)S(1)} %pad_maximum_fusion.6), channel_id=1, source_target_pairs={{0,3},{1,2},{2,1},{3,0},{4,7},{5,6},{6,5},{7,4},{8,11},{9,10},{10,... | collective-permute-start | bytes 393224 | tf_op jit(solution)/shard_map/ppermute | solution.py:60
  17.9 5.5 %collective-permute-done.2 = bf16[32,2048]{1,0:T(8,128)(2,1)S(1)} collective-permute-done((bf16[32,2048]{1,0:T(8,128)(2,1)S(1)}, bf16[32,2048]{1,0:T(8,128)(2,1)S(1)}, u32[]{:S(2)}, u32[]{:S(2)}) %collective-permute-start.2) | collective-permute-done | bytes 131104 | tf_op jit(solution)/shard_map/ppermute | solution.py:60
  26.1 3.1 %collective-permute-start.7 = (bf16[32,4096]{1,0:T(8,128)(2,1)S(1)}, bf16[32,4096]{1,0:T(8,128)(2,1)S(1)}, u32[]{:S(2)}, u32[]{:S(2)}) collective-permute-start(bf16[32,4096]{1,0:T(8,128)(2,1)S(1)} %maximum_select_fusion.8), channel_id=1, source_target_pairs={{0,12},{1,13},{2,14},{3,15},{4,0},{5,1},{6,2},{7,3},{8,4},{9,5},{1... | collective-permute-start | bytes 786440 | tf_op jit(solution)/shard_map/ppermute | solution.py:60
  32.6 3.3 %collective-permute-done.7 = bf16[32,4096]{1,0:T(8,128)(2,1)S(1)} collective-permute-done((bf16[32,4096]{1,0:T(8,128)(2,1)S(1)}, bf16[32,4096]{1,0:T(8,128)(2,1)S(1)}, u32[]{:S(2)}, u32[]{:S(2)}) %collective-permute-start.7) | collective-permute-done | bytes 262176 | tf_op jit(solution)/shard_map/ppermute | solution.py:60
  37.4 2.5 %collective-permute-done.9 = bf16[32,4096]{1,0:T(8,128)(2,1)S(1)} collective-permute-done((bf16[32,4096]{1,0:T(8,128)(2,1)S(1)}, bf16[32,4096]{1,0:T(8,128)(2,1)S(1)}, u32[]{:S(2)}, u32[]{:S(2)}) %collective-permute-start.9) | collective-permute-done | bytes 262176 | tf_op jit(solution)/shard_map/ppermute | solution.py:60
  39.9 5.6 %collective-permute-start.10 = (bf16[128,4096]{1,0:T(8,128)(2,1)S(1)}, bf16[128,4096]{1,0:T(8,128)(2,1)S(1)}, u32[]{:S(2)}, u32[]{:S(2)}) collective-permute-start(bf16[128,4096]{1,0:T(8,128)(2,1)S(1)} %constant_dynamic-update-slice_fusion.refs_0_), channel_id=1, source_target_pairs={{0,48},{1,49},{2,50},{3,51},{4,52},{5,53},{6,54},{7,55},{8,56},{9,... | collective-permute-start | bytes 3145736 | tf_op jit(solution)/shard_map/ppermute | solution.py:60
  49.2 8.7 %collective-permute-done.3 = bf16[128,2048]{1,0:T(8,128)(2,1)S(1)} collective-permute-done((bf16[128,2048]{1,0:T(8,128)(2,1)S(1)}, bf16[128,2048]{1,0:T(8,128)(2,1)S(1)}, u32[]{:S(2)}, u32[]{:S(2)}) %collective-permute-start.3) | collective-permute-done | bytes 524320 | tf_op jit(solution)/shard_map/ppermute | solution.py:211
  61.7 3.8 %collective-permute-start.19 = (bf16[64,4096]{1,0:T(8,128)(2,1)S(1)}, bf16[64,4096]{1,0:T(8,128)(2,1)S(1)}, u32[]{:S(2)}, u32[]{:S(2)}) collective-permute-start(bf16[64,4096]{1,0:T(8,128)(2,1)S(1)} %slice.72), channel_id=1, source_target_pairs={{0,48},{1,49},{2,50},{3,51},{4,52},{5,53},{6,54},{7,55},{8,56},{9,... | collective-permute-start | bytes 1572872 | tf_op jit(solution)/shard_map/ppermute | solution.py:60
  65.9 4.5 %collective-permute-done.12.refs_3_ = bf16[128,4096]{1,0:T(8,128)(2,1)S(1)} collective-permute-done((bf16[128,4096]{1,0:T(8,128)(2,1)S(1)}, bf16[128,4096]{1,0:T(8,128)(2,1)S(1)}, u32[]{:S(2)}, u32[]{:S(2)}) %collective-permute-start.12) | collective-permute-done | bytes 1048608 | tf_op jit(solution)/shard_map/ppermute | solution.py:60
  74.6 3.7 %collective-permute-done.13 = bf16[384,256]{1,0:T(8,128)(2,1)S(1)} collective-permute-done((bf16[384,256]{1,0:T(8,128)(2,1)S(1)}, bf16[384,256]{1,0:T(8,128)(2,1)S(1)}, u32[]{:S(2)}, u32[]{:S(2)}) %collective-permute-start.13) | collective-permute-done | bytes 196640 | tf_op jit(solution)/shard_map/ppermute | solution.py:230
  78.3 2.5 %convolution_convert_fusion = bf16[256,2048]{1,0:T(8,128)(2,1)S(1)} fusion(bf16[384,256]{1,0:T(8,128)(2,1)S(1)} %collective-permute-done.13, bf16[384,256]{1,0:T(8,128)(2,1)S(1)} %fusion.30, bf16[128,2048]{1,0:T(8,128)(2,1)S(1)} %collective-permute-done.16, bf16[128,2048]{1,0:T(8,128)(2,1)S(1)} %collective-permute-done.15, ...), kind=kOutput, calls=%fused_computation.3 | convolution fusion | flops 548405248 | bytes 3538944 | tf_op jit(solution)/shard_map/dot_general | solution.py:32
  82.0 4.6 %collective-permute-done.20 = bf16[64,4096]{1,0:T(8,128)(2,1)S(1)} collective-permute-done((bf16[64,4096]{1,0:T(8,128)(2,1)S(1)}, bf16[64,4096]{1,0:T(8,128)(2,1)S(1)}, u32[]{:S(2)}, u32[]{:S(2)}) %collective-permute-start.20) | collective-permute-done | bytes 524320 | tf_op jit(solution)/shard_map/ppermute | solution.py:60
  89.5 3.2 %collective-permute-start.18 = (bf16[128,2048]{1,0:T(8,128)(2,1)S(1)}, bf16[128,2048]{1,0:T(8,128)(2,1)S(1)}, u32[]{:S(2)}, u32[]{:S(2)}) collective-permute-start(bf16[128,2048]{1,0:T(8,128)(2,1)S(1)} %get-tuple-element.20), channel_id=1, source_target_pairs={{0,48},{1,49},{2,50},{3,51},{4,52},{5,53},{6,54},{7,55},{8,56},{9,... | collective-permute-start | bytes 1572872 | tf_op jit(solution)/shard_map/ppermute | solution.py:60
  95.8 2.1 %fusion.8 = f32[256,2048]{1,0:T(8,128)} fusion(bf16[256,512]{1,0:T(8,128)(2,1)S(1)} %fusion.17, bf16[512,4096]{1,0:T(8,128)(2,1)S(1)} %copy-done.6, s32[]{:T(128)S(6)} %select_n.310), kind=kOutput, calls=%fused_computation.16 | convolution fusion | flops 536870912 | bytes 4456452 | tf_op jit(solution)/shard_map/dot_general | solution.py:32
  99.9 5.2 %collective-permute-done.18 = bf16[128,2048]{1,0:T(8,128)(2,1)S(1)} collective-permute-done((bf16[128,2048]{1,0:T(8,128)(2,1)S(1)}, bf16[128,2048]{1,0:T(8,128)(2,1)S(1)}, u32[]{:S(2)}, u32[]{:S(2)}) %collective-permute-start.18) | collective-permute-done | bytes 524320 | tf_op jit(solution)/shard_map/ppermute | solution.py:60
  105.8 3.2 %fusion.94 = (bf16[128,2048]{1,0:T(8,128)(2,1)S(1)}, f32[128,2048]{1,0:T(8,128)}) fusion(bf16[128,2048]{1,0:T(8,128)(2,1)S(1)} %collective-permute-done.22, bf16[128,2048]{1,0:T(8,128)(2,1)S(1)} %collective-permute-done.18, bf16[128,2048]{1,0:T(8,128)(2,1)S(1)} %collective-permute-done.17, bf16[128,2048]{1,0:T(8,128)(2,1)S(1)} %collective-permute-done.16, ...), kind=kOutput, calls=%fused_computation.175 | convolution fusion | flops 281018368 | bytes 5636096 | tf_op jit(solution)/shard_map/dot_general | solution.py:32
  109.8 2.5 %collective-permute-start.23 = (bf16[32,2048]{1,0:T(8,128)(2,1)}, bf16[32,2048]{1,0:T(8,128)(2,1)S(1)}, u32[]{:S(2)}, u32[]{:S(2)}) collective-permute-start(bf16[32,2048]{1,0:T(8,128)(2,1)} %get-tuple-element.27), channel_id=1, source_target_pairs={{0,4},{1,5},{2,6},{3,7},{4,8},{5,9},{6,10},{7,11},{8,12},{9,13},{1... | collective-permute-start | bytes 393224 | tf_op jit(solution)/shard_map/ppermute | solution.py:60
  120.7 4.4 %convolution_add_fusion = f32[256,2048]{1,0:T(8,128)} fusion(f32[256,2048]{1,0:T(8,128)} %collective-permute-done.5, bf16[256,512]{1,0:T(8,128)(2,1)S(1)} %copy-done.9, bf16[512,4096]{1,0:T(8,128)(2,1)} %param.11, s32[]{:T(128)S(6)} %select_n.309), kind=kOutput, calls=%fused_computation.2 | convolution fusion | flops 537395200 | bytes 6553604 | tf_op jit(solution)/shard_map/dot_general | solution.py:32
  125.1 10.7 %shard_map.112 = (bf16[128,4096]{1,0:T(8,128)(2,1)}, bf16[128,1024]{1,0:T(8,128)(2,1)}) custom-call(f32[1024,128]{1,0:T(8,128)} %bitcast.29, bf16[128,4096]{1,0:T(8,128)(2,1)} %weight_ref.1, bf16[1024,4096]{1,0:T(8,128)(2,1)} %all-gather.2.cloned.1.call-done.back_ref, s32[1,1024]{1,0:T(1,128)} %reshape.331.places_ref), custom_call_target="tpu_custom_call" | custom-call | flops 2147483648 | bytes 10485760 | tf_op jit(solution)/shard_map/pallas_call | solution.py:98
  136.8 2.1 %dynamic-slice_convert_fusion = bf16[256,1024]{1,0:T(8,128)(2,1)} fusion(f32[256,2048]{1,0:T(8,128)} %convolution_add_fusion, s32[]{:T(128)S(6)} %select_n.312), kind=kLoop, calls=%fused_computation.23 | loop fusion | bytes 1048580 | tf_op jit(solution)/shard_map/convert_element_type | solution.py:219
  141.9 8.4 %shard_map.113 = bf16[4096,128]{1,0:T(8,128)(2,1)} custom-call(bf16[128,4096]{1,0:T(8,128)(2,1)} %copy-done.4, bf16[128,4096]{1,0:T(8,128)(2,1)} %copy-done.1, bf16[128,4096]{1,0:T(8,128)(2,1)} %copy-done.3, bf16[128,4096]{1,0:T(8,128)(2,1)} %copy-done.2, bf16[128,4096]{1,0:T(8,128)(2,1)} %collective-permute-done.29.refs_4_, ...), custom_call_target="tpu_custom_call" | custom-call | flops 1073741824 | bytes 9437184 | tf_op jit(solution)/shard_map/pallas_call | solution.py:136
  150.2 4.5 %collective-permute-done.6 = bf16[256,1024]{1,0:T(8,128)(2,1)} collective-permute-done((bf16[256,1024]{1,0:T(8,128)(2,1)}, bf16[256,1024]{1,0:T(8,128)(2,1)}, u32[]{:S(2)}, u32[]{:S(2)}) %collective-permute-start.6) | collective-permute-done | bytes 524320 | tf_op jit(solution)/shard_map/ppermute | solution.py:236
  154.8 2.8 %add_convert_fusion = bf16[256,1024]{1,0:T(8,128)(2,1)} fusion(bf16[256,1024]{1,0:T(8,128)(2,1)} %collective-permute-done.6, f32[256,2048]{1,0:T(8,128)} %convolution_add_fusion, s32[]{:T(128)S(6)} %select_n.311, f32[16,1024]{1,0:T(8,128)S(1)} %collective-permute-done.28, f32[16,1024]{1,0:T(8,128)S(1)} %get-tuple-element.34, f32[32]{0:T(128)S(1)} %copy-done.12, ...), kind=kOutput, calls=%fused_computation.21 | convolution fusion | flops 101851136 | bytes 2228485 | tf_op jit(solution)/shard_map/dot_general | solution.py:287
  (130 shorter events, 48.4 us)
Async XLA Ops:
  7.2 117.9 %all-gather.2.cloned.1.call-start = ((), (), s32[]{:S(2)}) async-start(), calls=%async_computation | async-start | bytes 8650752 | tf_op jit(solution)/shard_map/all_gather | solution.py:190
  14.4 9.0 %collective-permute-start.2 = (bf16[32,2048]{1,0:T(8,128)(2,1)S(1)}, bf16[32,2048]{1,0:T(8,128)(2,1)S(1)}, u32[]{:S(2)}, u32[]{:S(2)}) collective-permute-start(bf16[32,2048]{1,0:T(8,128)(2,1)S(1)} %pad_maximum_fusion.6), channel_id=1, source_target_pairs={{0,3},{1,2},{2,1},{3,0},{4,7},{5,6},{6,5},{7,4},{8,11},{9,10},{10,... | collective-permute-start | bytes 393224 | tf_op jit(solution)/shard_map/ppermute | solution.py:60
  24.4 33.5 %collective-permute-start.11 = (bf16[4096,128]{1,0:T(8,128)(2,1)}, bf16[4096,128]{1,0:T(8,128)(2,1)}, u32[]{:S(2)}, u32[]{:S(2)}) collective-permute-start(bf16[4096,128]{1,0:T(8,128)(2,1)} %param.12), channel_id=1, source_target_pairs={{0,64},{64,0},{1,65},{65,1},{2,66},{66,2},{3,67},{67,3},{4,68},{68... | collective-permute-start | bytes 3145736 | tf_op jit(solution)/shard_map/ppermute | solution.py:201
  26.1 9.8 %collective-permute-start.7 = (bf16[32,4096]{1,0:T(8,128)(2,1)S(1)}, bf16[32,4096]{1,0:T(8,128)(2,1)S(1)}, u32[]{:S(2)}, u32[]{:S(2)}) collective-permute-start(bf16[32,4096]{1,0:T(8,128)(2,1)S(1)} %maximum_select_fusion.8), channel_id=1, source_target_pairs={{0,12},{1,13},{2,14},{3,15},{4,0},{5,1},{6,2},{7,3},{8,4},{9,5},{1... | collective-permute-start | bytes 786440 | tf_op jit(solution)/shard_map/ppermute | solution.py:60
  29.8 10.1 %collective-permute-start.9 = (bf16[32,4096]{1,0:T(8,128)(2,1)S(1)}, bf16[32,4096]{1,0:T(8,128)(2,1)S(1)}, u32[]{:S(2)}, u32[]{:S(2)}) collective-permute-start(bf16[32,4096]{1,0:T(8,128)(2,1)S(1)} %maximum_select_fusion.8), channel_id=1, source_target_pairs={{0,4},{1,5},{2,6},{3,7},{4,8},{5,9},{6,10},{7,11},{8,12},{9,13},{1... | collective-permute-start | bytes 786440 | tf_op jit(solution)/shard_map/ppermute | solution.py:60
  30.9 16.4 %collective-permute-start.15 = (bf16[128,2048]{1,0:T(8,128)(2,1)S(1)}, bf16[128,2048]{1,0:T(8,128)(2,1)S(1)}, u32[]{:S(2)}, u32[]{:S(2)}) collective-permute-start(bf16[128,2048]{1,0:T(8,128)(2,1)S(1)} %pad_maximum_fusion.2), channel_id=1, source_target_pairs={{0,1},{1,0},{2,3},{3,2},{4,5},{5,4},{6,7},{7,6},{8,9},{9,8},{10,11... | collective-permute-start | bytes 1572872 | tf_op jit(solution)/shard_map/ppermute | solution.py:205
  35.9 22.0 %collective-permute-start.3 = (bf16[128,2048]{1,0:T(8,128)(2,1)S(1)}, bf16[128,2048]{1,0:T(8,128)(2,1)S(1)}, u32[]{:S(2)}, u32[]{:S(2)}) collective-permute-start(bf16[128,2048]{1,0:T(8,128)(2,1)S(1)} %constant_dynamic-slice_fusion.6), channel_id=1, source_target_pairs={{0,1},{1,0},{2,3},{3,2},{4,5},{5,4},{6,7},{7,6},{8,9},{9,8},{10,11... | collective-permute-start | bytes 1572872 | tf_op jit(solution)/shard_map/ppermute | solution.py:211
  39.9 21.7 %collective-permute-start.10 = (bf16[128,4096]{1,0:T(8,128)(2,1)S(1)}, bf16[128,4096]{1,0:T(8,128)(2,1)S(1)}, u32[]{:S(2)}, u32[]{:S(2)}) collective-permute-start(bf16[128,4096]{1,0:T(8,128)(2,1)S(1)} %constant_dynamic-update-slice_fusion.refs_0_), channel_id=1, source_target_pairs={{0,48},{1,49},{2,50},{3,51},{4,52},{5,53},{6,54},{7,55},{8,56},{9,... | collective-permute-start | bytes 3145736 | tf_op jit(solution)/shard_map/ppermute | solution.py:60
  45.5 29.1 %collective-permute-start.14 = (bf16[128,2048]{1,0:T(8,128)(2,1)S(1)}, bf16[128,2048]{1,0:T(8,128)(2,1)S(1)}, u32[]{:S(2)}, u32[]{:S(2)}) collective-permute-start(bf16[128,2048]{1,0:T(8,128)(2,1)S(1)} %pad_maximum_fusion.1), channel_id=1, source_target_pairs={{0,64},{64,0},{1,65},{65,1},{2,66},{66,2},{3,67},{67,3},{4,68},{68... | collective-permute-start | bytes 1572872 | tf_op jit(solution)/shard_map/ppermute | solution.py:206
  47.3 23.1 %collective-permute-start.12 = (bf16[128,4096]{1,0:T(8,128)(2,1)S(1)}, bf16[128,4096]{1,0:T(8,128)(2,1)S(1)}, u32[]{:S(2)}, u32[]{:S(2)}) collective-permute-start(bf16[128,4096]{1,0:T(8,128)(2,1)S(1)} %constant_dynamic-update-slice_fusion.refs_0_), channel_id=1, source_target_pairs={{0,16},{1,17},{2,18},{3,19},{4,20},{5,21},{6,22},{7,23},{8,24},{9,... | collective-permute-start | bytes 3145736 | tf_op jit(solution)/shard_map/ppermute | solution.py:60
  57.9 16.7 %collective-permute-start.16 = (bf16[128,2048]{1,0:T(8,128)(2,1)S(1)}, bf16[128,2048]{1,0:T(8,128)(2,1)S(1)}, u32[]{:S(2)}, u32[]{:S(2)}) collective-permute-start(bf16[128,2048]{1,0:T(8,128)(2,1)S(1)} %collective-permute-done.15), channel_id=1, source_target_pairs={{0,64},{64,0},{1,65},{65,1},{2,66},{66,2},{3,67},{67,3},{4,68},{68... | collective-permute-start | bytes 1572872 | tf_op jit(solution)/shard_map/ppermute | solution.py:207
  61.7 20.3 %collective-permute-start.19 = (bf16[64,4096]{1,0:T(8,128)(2,1)S(1)}, bf16[64,4096]{1,0:T(8,128)(2,1)S(1)}, u32[]{:S(2)}, u32[]{:S(2)}) collective-permute-start(bf16[64,4096]{1,0:T(8,128)(2,1)S(1)} %slice.72), channel_id=1, source_target_pairs={{0,48},{1,49},{2,50},{3,51},{4,52},{5,53},{6,54},{7,55},{8,56},{9,... | collective-permute-start | bytes 1572872 | tf_op jit(solution)/shard_map/ppermute | solution.py:60
  72.6 14.0 %collective-permute-start.20 = (bf16[64,4096]{1,0:T(8,128)(2,1)S(1)}, bf16[64,4096]{1,0:T(8,128)(2,1)S(1)}, u32[]{:S(2)}, u32[]{:S(2)}) collective-permute-start(bf16[64,4096]{1,0:T(8,128)(2,1)S(1)} %slice.73), channel_id=1, source_target_pairs={{0,16},{1,17},{2,18},{3,19},{4,20},{5,21},{6,22},{7,23},{8,24},{9,... | collective-permute-start | bytes 1572872 | tf_op jit(solution)/shard_map/ppermute | solution.py:60
  89.3 10.6 %collective-permute-start.17 = (bf16[128,2048]{1,0:T(8,128)(2,1)S(1)}, bf16[128,2048]{1,0:T(8,128)(2,1)S(1)}, u32[]{:S(2)}, u32[]{:S(2)}) collective-permute-start(bf16[128,2048]{1,0:T(8,128)(2,1)S(1)} %get-tuple-element.19), channel_id=1, source_target_pairs={{0,16},{1,17},{2,18},{3,19},{4,20},{5,21},{6,22},{7,23},{8,24},{9,... | collective-permute-start | bytes 1572872 | tf_op jit(solution)/shard_map/ppermute | solution.py:60
  89.5 15.5 %collective-permute-start.18 = (bf16[128,2048]{1,0:T(8,128)(2,1)S(1)}, bf16[128,2048]{1,0:T(8,128)(2,1)S(1)}, u32[]{:S(2)}, u32[]{:S(2)}) collective-permute-start(bf16[128,2048]{1,0:T(8,128)(2,1)S(1)} %get-tuple-element.20), channel_id=1, source_target_pairs={{0,48},{1,49},{2,50},{3,51},{4,52},{5,53},{6,54},{7,55},{8,56},{9,... | collective-permute-start | bytes 1572872 | tf_op jit(solution)/shard_map/ppermute | solution.py:60
  93.9 11.9 %collective-permute-start.22 = (bf16[128,2048]{1,0:T(8,128)(2,1)S(1)}, bf16[128,2048]{1,0:T(8,128)(2,1)S(1)}, u32[]{:S(2)}, u32[]{:S(2)}) collective-permute-start(bf16[128,2048]{1,0:T(8,128)(2,1)S(1)} %convolution_convert_fusion.1), channel_id=1, source_target_pairs={{0,32},{1,33},{2,34},{3,35},{4,36},{5,37},{6,38},{7,39},{8,40},{9,... | collective-permute-start | bytes 1572872 | tf_op jit(solution)/shard_map/ppermute | solution.py:60
  98.0 22.7 %collective-permute-start.5 = (f32[256,2048]{1,0:T(8,128)}, f32[256,2048]{1,0:T(8,128)}, u32[]{:S(2)}, u32[]{:S(2)}) collective-permute-start(f32[256,2048]{1,0:T(8,128)} %fusion.8), channel_id=1, source_target_pairs={{0,64},{64,0},{1,65},{65,1},{2,66},{66,2},{3,67},{67,3},{4,68},{68... | collective-permute-start | bytes 6291464 | tf_op jit(solution)/shard_map/ppermute | solution.py:217
  99.4 16.3 %collective-permute-start.26 = (f32[512,128]{1,0:T(8,128)}, f32[512,128]{1,0:T(8,128)}, u32[]{:S(2)}, u32[]{:S(2)}) collective-permute-start(f32[512,128]{1,0:T(8,128)} %get-tuple-element.26), channel_id=1, source_target_pairs={{0,64},{64,0},{1,65},{65,1},{2,66},{66,2},{3,67},{67,3},{4,68},{68... | collective-permute-start | bytes 786440 | tf_op jit(solution)/shard_map/ppermute | solution.py:270
  115.7 26.0 %collective-permute-start.29 = (bf16[128,4096]{1,0:T(8,128)(2,1)}, bf16[128,4096]{1,0:T(8,128)(2,1)}, u32[]{:S(2)}, u32[]{:S(2)}) collective-permute-start(bf16[128,4096]{1,0:T(8,128)(2,1)} %copy-done.4), channel_id=1, source_target_pairs={{0,64},{64,0},{1,65},{65,1},{2,66},{66,2},{3,67},{67,3},{4,68},{68... | collective-permute-start | bytes 3145736 | tf_op jit(solution)/shard_map/ppermute | solution.py:282
  117.6 24.2 %collective-permute-start.30 = (bf16[128,4096]{1,0:T(8,128)(2,1)S(1)}, bf16[128,4096]{1,0:T(8,128)(2,1)}, u32[]{:S(2)}, u32[]{:S(2)}) collective-permute-start(bf16[128,4096]{1,0:T(8,128)(2,1)S(1)} %collective-permute-done.10.refs_1_), channel_id=1, source_target_pairs={{0,64},{64,0},{1,65},{65,1},{2,66},{66,2},{3,67},{67,3},{4,68},{68... | collective-permute-start | bytes 3145736 | tf_op jit(solution)/shard_map/ppermute | solution.py:282
  119.1 22.8 %collective-permute-start.32 = (bf16[128,4096]{1,0:T(8,128)(2,1)S(1)}, bf16[128,4096]{1,0:T(8,128)(2,1)}, u32[]{:S(2)}, u32[]{:S(2)}) collective-permute-start(bf16[128,4096]{1,0:T(8,128)(2,1)S(1)} %collective-permute-done.12.refs_3_), channel_id=1, source_target_pairs={{0,64},{64,0},{1,65},{65,1},{2,66},{66,2},{3,67},{67,3},{4,68},{68... | collective-permute-start | bytes 3145736 | tf_op jit(solution)/shard_map/ppermute | solution.py:282
  119.1 22.8 %collective-permute-start.31 = (bf16[128,4096]{1,0:T(8,128)(2,1)}, bf16[128,4096]{1,0:T(8,128)(2,1)}, u32[]{:S(2)}, u32[]{:S(2)}) collective-permute-start(bf16[128,4096]{1,0:T(8,128)(2,1)} %copy-done.3), channel_id=1, source_target_pairs={{0,64},{64,0},{1,65},{65,1},{2,66},{66,2},{3,67},{67,3},{4,68},{68... | collective-permute-start | bytes 3145736 | tf_op jit(solution)/shard_map/ppermute | solution.py:282
  140.2 14.6 %collective-permute-start.6 = (bf16[256,1024]{1,0:T(8,128)(2,1)}, bf16[256,1024]{1,0:T(8,128)(2,1)}, u32[]{:S(2)}, u32[]{:S(2)}) collective-permute-start(bf16[256,1024]{1,0:T(8,128)(2,1)} %dynamic-slice_convert_fusion), channel_id=1, source_target_pairs={{0,1},{1,0},{2,3},{3,2},{4,5},{5,4},{6,7},{7,6},{8,9},{9,8},{10,11... | collective-permute-start | bytes 1572872 | tf_op jit(solution)/shard_map/ppermute | solution.py:236
  141.8 13.0 %collective-permute-start.28 = (f32[16,1024]{1,0:T(8,128)S(1)}, f32[16,1024]{1,0:T(8,128)S(1)}, u32[]{:S(2)}, u32[]{:S(2)}) collective-permute-start(f32[16,1024]{1,0:T(8,128)S(1)} %get-tuple-element.35), channel_id=1, source_target_pairs={{0,64},{64,0},{1,65},{65,1},{2,66},{66,2},{3,67},{67,3},{4,68},{68... | collective-permute-start | bytes 196616 | tf_op jit(solution)/shard_map/ppermute | solution.py:284
  (24 other events, 270.1 us)
Sparse Core Ops, SparseCore 0:
  24.5 61.2 all-gather.1

commit v2 on v1

--- a/solution.py
+++ b/solution.py
@@ -13,6 +13,8 @@
 
 swap = [(0, 1), (1, 0)]
 axes = ("b", "z", "y", "xl", "xh")
+grant = 20 << 20
+whole = pl.BlockSpec(memory_space=pltpu.VMEM)
 sizes = (2, 4, 4, 2, 2)
 
 
@@ -71,51 +73,30 @@
 def grad_out_of(pre, weight, back, places, tile=512):
     rows, features = back.shape
     units = pre.shape[1]
-    last = features // tile - 1
-
-    def kernel(pre_ref, weight_ref, back_ref, places_ref, out_ref, slope_ref, hidden, total):
-        step = pl.program_id(0)
-
-        @pl.when(step == 0)
-        def _():
-            hidden[...] = gelu_tanh(pre_ref[...]).T.astype(hidden.dtype)
-            total[...] = jnp.zeros_like(total)
-
-        tiles = back_ref[...]
-        out_ref[...] = dot(hidden[...], tiles).astype(out_ref.dtype)
-        total[...] += general(tiles, weight_ref[...], (1,), (1,))
-
-        @pl.when(step == last)
-        def _():
-            slope = (total[...] * gelu_slope(pre_ref[...])).T.astype(slope_ref.dtype)
-            for at in range(0, rows, 256):
-                target = at + lax.broadcasted_iota(jnp.int32, (256, rows), 0)
-                moves = (target == places_ref[...]).astype(jnp.float32).astype(slope.dtype)
-                slope_ref[:, at : at + 256] = general(slope, moves, (1,), (1,)).astype(
-                    slope_ref.dtype
-                )
+
+    def kernel(pre_ref, weight_ref, back_ref, places_ref, out_ref, slope_ref, total):
+        hidden = gelu_tanh(pre_ref[...]).T.astype(jnp.bfloat16)
+        for at in range(0, features, tile):
+            tiles = back_ref[:, at : at + tile]
+            out_ref[:, at : at + tile] = dot(hidden, tiles).astype(out_ref.dtype)
+            term = general(tiles, weight_ref[:, at : at + tile], (1,), (1,))
+            total[...] = total[...] + term if at else term
+        slope = (total[...] * gelu_slope(pre_ref[...])).T.astype(slope_ref.dtype)
+        for at in range(0, rows, 256):
+            target = at + lax.broadcasted_iota(jnp.int32, (256, rows), 0)
+            moves = (target == places_ref[...]).astype(jnp.float32).astype(slope.dtype)
+            slope_ref[:, at : at + 256] = general(slope, moves, (1,), (1,)).astype(slope_ref.dtype)
 
     return pl.pallas_call(
         kernel,
-        grid=(last + 1,),
-        in_specs=[
-            pl.BlockSpec((rows, units), lambda i: (0, 0)),
-            pl.BlockSpec((units, tile), lambda i: (0, i)),
-            pl.BlockSpec((rows, tile), lambda i: (0, i)),
-            pl.BlockSpec((1, rows), lambda i: (0, 0)),
-        ],
-        out_specs=[
-            pl.BlockSpec((units, tile), lambda i: (0, i)),
-            pl.BlockSpec((units, rows), lambda i: (0, 0)),
-        ],
+        in_specs=[whole] * 4,
+        out_specs=[whole] * 2,
         out_shape=[
             jax.ShapeDtypeStruct((units, features), jnp.bfloat16),
             jax.ShapeDtypeStruct((units, rows), jnp.bfloat16),
         ],
-        scratch_shapes=[
-            pltpu.VMEM((units, rows), jnp.bfloat16),
-            pltpu.VMEM((rows, units), jnp.float32),
-        ],
+        scratch_shapes=[pltpu.VMEM((rows, units), jnp.float32)],
+        compiler_params=pltpu.CompilerParams(vmem_limit_bytes=grant),
         cost_estimate=pl.CostEstimate(
             flops=4 * rows * units * features,
             bytes_accessed=2 * (rows * features + 2 * units * features),
@@ -125,21 +106,21 @@
 
 
 def grad_in_of(sheets, slope, tile=512):
-    tall, features = sheets[0].shape
+    features = sheets[0].shape[1]
     units, rows = slope.shape
 
     def kernel(*refs):
         slope_ref, out_ref = refs[-2:]
-        tiles = jnp.concatenate([ref[...] for ref in refs[:-2]], axis=0)
-        out_ref[...] = dot(slope_ref[...], tiles).T.astype(out_ref.dtype)
+        for at in range(0, features, tile):
+            tiles = jnp.concatenate([ref[:, at : at + tile] for ref in refs[:-2]], axis=0)
+            out_ref[at : at + tile, :] = dot(slope_ref[...], tiles).T.astype(out_ref.dtype)
 
     return pl.pallas_call(
         kernel,
-        grid=(features // tile,),
-        in_specs=[pl.BlockSpec((tall, tile), lambda i: (0, i)) for _ in sheets]
-        + [pl.BlockSpec((units, rows), lambda i: (0, 0))],
-        out_specs=pl.BlockSpec((tile, units), lambda i: (i, 0)),
+        in_specs=[whole] * (len(sheets) + 1),
+        out_specs=whole,
         out_shape=jax.ShapeDtypeStruct((features, units), jnp.bfloat16),
+        compiler_params=pltpu.CompilerParams(vmem_limit_bytes=grant),
         cost_estimate=pl.CostEstimate(
             flops=2 * rows * units * features,
             bytes_accessed=2 * (rows * features + units * features),
@@ -209,7 +190,8 @@
 
     sent = part(later_tokens, core, rows // 2, 0)
     got = lax.ppermute(sent, "xh", swap)
-    other = ordered(core == 0, got, lax.ppermute(got, "b", swap), 0)
+    got_tokens = lax.ppermute(got, "b", swap)
+    other = ordered(core == 0, got, got_tokens, 0)
     whole = ordered(side == 0, tokens, other, 1)
     light_hidden = gelu_tanh(dot(whole, light_in)).astype(jnp.bfloat16)
     theirs = dot(light_hidden, part(light_out, 1 - core, width, 1))
@@ -233,9 +215,10 @@
     late = jnp.concatenate([late, across], axis=1)
     near = dot(early[: 2 * tall], group_weight).astype(jnp.bfloat16)
     far = dot(late, group_weight).astype(jnp.bfloat16)
+    far, back = lax.optimization_barrier((far, back))
     light_got = lax.ppermute(light_given, "xh", swap)
     light_share = light_kept + light_got.astype(jnp.float32)
-    own = dot(early[2 * tall :], group_weight)
+    own = lax.optimization_barrier(dot(early[2 * tall :], group_weight))
     from_before = moved(near[:tall], third(1))
     from_after = moved(near[tall:], third(-1))
     from_facing = moved(far, third(2))

time: 165 us -> 149 us (0.903)
  Pallas kernels: 19.1 us -> 8.27 us
  matrix products: 19.6 us -> 16 us
  waiting for transfers between devices: 50.7 us -> 47.2 us
  starting transfers between devices: 42.3 us -> 45.7 us
  local copies, waits for them, and re-layouts: 12.3 us -> 10.2 us
    pallas_call x2, Pallas kernels: 19.1 us -> 8.27 us  [the longest x1 5.94 us: grad_out_of(): pl.pallas_call(kernel, in_specs=[whole] * 4, out_specs=[whole] * 2, out_s...]
    ppermute x16, waiting for transfers between devices: 29.8 us -> 24.2 us  [moved(): lax.ppermute(x, axes, [(number(p), number(step(*p))) for p in places])]
    ppermute x1, waiting for transfers between devices: 4.54 us -> 9.01 us  [per_device(): light_got = lax.ppermute(light_given, 'xh', swap)]
    ppermute x1, waiting for transfers between devices: 3.69 us -> 0.01 us  [per_device(): early = jnp.concatenate([early, lax.ppermute(early, 'xh', swap)], axis=1)]
    dot_general x10, matrix products: 16.1 us -> 13.8 us  [dot(): return jnp.dot(left, right, preferred_element_type=jnp.float32)]
    ppermute x1, starting transfers between devices: 1.52 us -> 3.57 us  [per_device(): across = lax.ppermute(late, 'xh', swap)]
    convert_element_type x1, local copies, waits for them, and re-layouts: 2.09 us -> 0.07 us  [per_device(): light_given = part(chip_terms, 1 - side, block, 1).astype(jnp.bfloat16)]
    ppermute x1, starting transfers between devices: 1.48 us -> 3.49 us  [per_device(): light_got = lax.ppermute(light_given, 'xh', swap)]
  transfers between devices with their start and end apart: 34 -> 34, of which waited for: 18 -> 14; matrix products, arithmetic and copies ran while one was open for 17% -> 16% of each run, Pallas kernels for 12% -> 6%
where the time goes in v2:
time: 149 us; the launch traced here: 148 us
  waiting for transfers between devices  47.2 us (32%)
  starting transfers between devices  45.7 us (31%)
  matrix products  16 us (11%)
  between operations  15.4 us (10%)
  local copies, waits for them, and re-layouts  10.2 us (7%)
  Pallas kernels  8.27 us (6%)
  other arithmetic  5.7 us (4%)
    ppermute x16, starting transfers between devices, moved(): lax.ppermute(x, axes, [(number(p), number(step(*p))) for p in places])  31.5 us
    ppermute x16, waiting for transfers between devices, moved(): lax.ppermute(x, axes, [(number(p), number(step(*p))) for p in places])  24.2 us
    dot_general x10, matrix products, dot(): return jnp.dot(left, right, preferred_element_type=jnp.float32)  13.8 us
    ppermute x1, waiting for transfers between devices, per_device(): light_got = lax.ppermute(light_given, 'xh', swap)  9.01 us
    ppermute x1, waiting for transfers between devices, per_device(): got = lax.ppermute(sent, 'xh', swap)  8.65 us
    pallas_call x1, Pallas kernels, grad_out_of(): pl.pallas_call(kernel, in_specs=[whole] * 4, out_specs=[whole] * 2, out_s...  5.94 us
    ppermute x1, starting transfers between devices, per_device(): across = lax.ppermute(late, 'xh', swap)  3.57 us
    ppermute x1, starting transfers between devices, per_device(): light_got = lax.ppermute(light_given, 'xh', swap)  3.49 us
  transfers between devices with their start and end apart: 34, of which 14 were waited for; matrix products, arithmetic and copies ran while one was open for 16% of the time, Pallas kernels for 6%

profile of v2, /device:TPU:0, one launch (start us, length us, event | category | flops | bytes accessed | tf_op | source)
XLA Modules:
  0.0 148.5 jit_solution(7603428844196312141)
XLA Ops:
  10.0 2.0 %gather_fusion = bf16[16,2048]{1,0:T(8,128)(2,1)S(1)} fusion(bf16[256,2048]{1,0:T(8,128)(2,1)} %param.9, s32[1024]{0:T(1024)S(1)} %pad_clamp_fusion), kind=kCustom, calls=%fused_computation | custom fusion | bytes 131136 | tf_op jit(solution)/shard_map/jit(_take)/gather | solution.py:161
  13.8 2.1 %collective-permute-start.2 = (bf16[32,2048]{1,0:T(8,128)(2,1)S(1)}, bf16[32,2048]{1,0:T(8,128)(2,1)S(1)}, u32[]{:S(2)}, u32[]{:S(2)}) collective-permute-start(bf16[32,2048]{1,0:T(8,128)(2,1)S(1)} %pad_maximum_fusion.6), channel_id=1, source_target_pairs={{0,3},{1,2},{2,1},{3,0},{4,7},{5,6},{6,5},{7,4},{8,11},{9,10},{10,... | collective-permute-start | bytes 393224 | tf_op jit(solution)/shard_map/ppermute | solution.py:62
  17.3 5.5 %collective-permute-done.2 = bf16[32,2048]{1,0:T(8,128)(2,1)S(1)} collective-permute-done((bf16[32,2048]{1,0:T(8,128)(2,1)S(1)}, bf16[32,2048]{1,0:T(8,128)(2,1)S(1)}, u32[]{:S(2)}, u32[]{:S(2)}) %collective-permute-start.2) | collective-permute-done | bytes 131104 | tf_op jit(solution)/shard_map/ppermute | solution.py:62
  25.7 3.1 %collective-permute-start.7 = (bf16[32,4096]{1,0:T(8,128)(2,1)S(1)}, bf16[32,4096]{1,0:T(8,128)(2,1)S(1)}, u32[]{:S(2)}, u32[]{:S(2)}) collective-permute-start(bf16[32,4096]{1,0:T(8,128)(2,1)S(1)} %maximum_select_fusion.8), channel_id=1, source_target_pairs={{0,12},{1,13},{2,14},{3,15},{4,0},{5,1},{6,2},{7,3},{8,4},{9,5},{1... | collective-permute-start | bytes 786440 | tf_op jit(solution)/shard_map/ppermute | solution.py:62
  32.2 3.2 %collective-permute-done.7 = bf16[32,4096]{1,0:T(8,128)(2,1)S(1)} collective-permute-done((bf16[32,4096]{1,0:T(8,128)(2,1)S(1)}, bf16[32,4096]{1,0:T(8,128)(2,1)S(1)}, u32[]{:S(2)}, u32[]{:S(2)}) %collective-permute-start.7) | collective-permute-done | bytes 262176 | tf_op jit(solution)/shard_map/ppermute | solution.py:62
  39.7 5.5 %collective-permute-start.10 = (bf16[128,4096]{1,0:T(8,128)(2,1)S(1)}, bf16[128,4096]{1,0:T(8,128)(2,1)S(1)}, u32[]{:S(2)}, u32[]{:S(2)}) collective-permute-start(bf16[128,4096]{1,0:T(8,128)(2,1)S(1)} %constant_dynamic-update-slice_fusion.refs_0_), channel_id=1, source_target_pairs={{0,48},{1,49},{2,50},{3,51},{4,52},{5,53},{6,54},{7,55},{8,56},{9,... | collective-permute-start | bytes 3145736 | tf_op jit(solution)/shard_map/ppermute | solution.py:62
  48.8 8.7 %collective-permute-done.3 = bf16[128,2048]{1,0:T(8,128)(2,1)S(1)} collective-permute-done((bf16[128,2048]{1,0:T(8,128)(2,1)S(1)}, bf16[128,2048]{1,0:T(8,128)(2,1)S(1)}, u32[]{:S(2)}, u32[]{:S(2)}) %collective-permute-start.3) | collective-permute-done | bytes 524320 | tf_op jit(solution)/shard_map/ppermute | solution.py:192
  63.5 6.7 %collective-permute-done.12.refs_3_ = bf16[128,4096]{1,0:T(8,128)(2,1)S(1)} collective-permute-done((bf16[128,4096]{1,0:T(8,128)(2,1)S(1)}, bf16[128,4096]{1,0:T(8,128)(2,1)S(1)}, u32[]{:S(2)}, u32[]{:S(2)}) %collective-permute-start.12) | collective-permute-done | bytes 1048608 | tf_op jit(solution)/shard_map/ppermute | solution.py:62
  70.9 2.2 %fusion.6 = f32[256,2048]{1,0:T(8,128)} fusion(bf16[256,512]{1,0:T(8,128)(2,1)S(1)} %fusion.15, bf16[512,4096]{1,0:T(8,128)(2,1)S(1)} %copy-done.7, s32[]{:T(128)S(6)} %select_n.310), kind=kOutput, calls=%fused_computation.13 | convolution fusion | flops 536870912 | bytes 4456452 | tf_op jit(solution)/shard_map/dot_general | solution.py:34
  73.1 4.6 %collective-permute-start.19 = (bf16[64,4096]{1,0:T(8,128)(2,1)S(1)}, bf16[64,4096]{1,0:T(8,128)(2,1)S(1)}, u32[]{:S(2)}, u32[]{:S(2)}) collective-permute-start(bf16[64,4096]{1,0:T(8,128)(2,1)S(1)} %slice.72), channel_id=1, source_target_pairs={{0,48},{1,49},{2,50},{3,51},{4,52},{5,53},{6,54},{7,55},{8,56},{9,... | collective-permute-start | bytes 1572872 | tf_op jit(solution)/shard_map/ppermute | solution.py:62
  78.1 2.6 %convolution_convert_fusion = bf16[256,2048]{1,0:T(8,128)(2,1)S(1)} fusion(bf16[384,256]{1,0:T(8,128)(2,1)S(1)} %collective-permute-done.13, bf16[384,256]{1,0:T(8,128)(2,1)S(1)} %fusion.28, bf16[128,2048]{1,0:T(8,128)(2,1)S(1)} %collective-permute-done.16, bf16[128,2048]{1,0:T(8,128)(2,1)S(1)} %collective-permute-done.15, ...), kind=kOutput, calls=%fused_computation.3 | convolution fusion | flops 548405248 | bytes 3538944 | tf_op jit(solution)/shard_map/dot_general | solution.py:34
  83.6 2.7 %collective-permute-start.18 = (bf16[128,2048]{1,0:T(8,128)(2,1)}, bf16[128,2048]{1,0:T(8,128)(2,1)}, u32[]{:S(2)}, u32[]{:S(2)}) collective-permute-start(bf16[128,2048]{1,0:T(8,128)(2,1)} %get-tuple-element.26), channel_id=1, source_target_pairs={{0,48},{1,49},{2,50},{3,51},{4,52},{5,53},{6,54},{7,55},{8,56},{9,... | collective-permute-start | bytes 1572872 | tf_op jit(solution)/shard_map/ppermute | solution.py:62
  86.3 2.2 %collective-permute-done.20 = bf16[64,4096]{1,0:T(8,128)(2,1)S(1)} collective-permute-done((bf16[64,4096]{1,0:T(8,128)(2,1)S(1)}, bf16[64,4096]{1,0:T(8,128)(2,1)S(1)}, u32[]{:S(2)}, u32[]{:S(2)}) %collective-permute-start.20) | collective-permute-done | bytes 524320 | tf_op jit(solution)/shard_map/ppermute | solution.py:62
  89.0 3.6 %collective-permute-start.21 = (bf16[128,256]{1,0:T(8,128)(2,1)S(1)}, bf16[128,256]{1,0:T(8,128)(2,1)S(1)}, u32[]{:S(2)}, u32[]{:S(2)}) collective-permute-start(bf16[128,256]{1,0:T(8,128)(2,1)S(1)} %get-tuple-element.42), channel_id=1, source_target_pairs={{0,1},{1,0},{2,3},{3,2},{4,5},{5,4},{6,7},{7,6},{8,9},{9,8},{10,11... | collective-permute-start | bytes 196616 | tf_op jit(solution)/shard_map/ppermute | solution.py:214
  96.3 2.1 %fusion.37 = f32[128,2048]{1,0:T(8,128)S(1)} fusion(bf16[384,256]{1,0:T(8,128)(2,1)} %copy-done.20, bf16[384,256]{1,0:T(8,128)(2,1)} %copy-done.14, bf16[128,2048]{1,0:T(8,128)(2,1)} %copy-done.19, bf16[128,2048]{1,0:T(8,128)(2,1)} %copy-done.17, bf16[128,2048]{1,0:T(8,128)(2,1)} %copy-done.18, bf16[128,1024]{1,0:T(8,128)(2,1)} %copy-done.9, ...), kind=kOutput, calls=%fused_computation.62 | convolution fusion | flops 279183360 | bytes 3538944 | tf_op jit(solution)/shard_map/dot_general | solution.py:34
  100.6 2.5 %convolution_add_fusion = f32[256,2048]{1,0:T(8,128)S(1)} fusion(f32[256,2048]{1,0:T(8,128)} %collective-permute-done.5, bf16[256,512]{1,0:T(8,128)(2,1)S(1)} %copy-done.13, bf16[512,4096]{1,0:T(8,128)(2,1)S(1)} %copy-done.8, s32[]{:T(128)S(6)} %select_n.309), kind=kOutput, calls=%fused_computation.2 | convolution fusion | flops 537395200 | bytes 6553604 | tf_op jit(solution)/shard_map/dot_general | solution.py:34
  103.2 3.9 %collective-permute-done.22 = bf16[128,2048]{1,0:T(8,128)(2,1)S(1)} collective-permute-done((bf16[128,2048]{1,0:T(8,128)(2,1)}, bf16[128,2048]{1,0:T(8,128)(2,1)S(1)}, u32[]{:S(2)}, u32[]{:S(2)}) %collective-permute-start.22) | collective-permute-done | bytes 524320 | tf_op jit(solution)/shard_map/ppermute | solution.py:62
  108.6 2.8 %collective-permute-start.23 = (bf16[32,2048]{1,0:T(8,128)(2,1)S(1)}, bf16[32,2048]{1,0:T(8,128)(2,1)S(1)}, u32[]{:S(2)}, u32[]{:S(2)}) collective-permute-start(bf16[32,2048]{1,0:T(8,128)(2,1)S(1)} %get-tuple-element.33), channel_id=1, source_target_pairs={{0,4},{1,5},{2,6},{3,7},{4,8},{5,9},{6,10},{7,11},{8,12},{9,13},{1... | collective-permute-start | bytes 393224 | tf_op jit(solution)/shard_map/ppermute | solution.py:62
  111.5 2.7 %collective-permute-start.25 = (bf16[32,2048]{1,0:T(8,128)(2,1)S(1)}, bf16[32,2048]{1,0:T(8,128)(2,1)S(1)}, u32[]{:S(2)}, u32[]{:S(2)}) collective-permute-start(bf16[32,2048]{1,0:T(8,128)(2,1)S(1)} %get-tuple-element.34), channel_id=1, source_target_pairs={{0,12},{1,13},{2,14},{3,15},{4,0},{5,1},{6,2},{7,3},{8,4},{9,5},{1... | collective-permute-start | bytes 393224 | tf_op jit(solution)/shard_map/ppermute | solution.py:62
  114.2 5.9 %shard_map.112 = (bf16[128,4096]{1,0:T(8,128)(2,1)}, bf16[128,1024]{1,0:T(8,128)(2,1)S(1)}) custom-call(f32[1024,128]{1,0:T(8,128)S(1)} %bitcast.31, bf16[128,4096]{1,0:T(8,128)(2,1)S(1)} %copy-done.6, bf16[1024,4096]{1,0:T(8,128)(2,1)S(1)} %bitcast.30, s32[1,1024]{1,0:T(1,128)S(1)} %reshape.331.places_ref), custom_call_target="tpu_custom_call" | custom-call | flops 2147483648 | bytes 10485760 | tf_op jit(solution)/shard_map/pallas_call | solution.py:90
  122.6 2.5 %collective-permute-done.27 = bf16[16,2048]{1,0:T(8,128)(2,1)S(1)} collective-permute-done((bf16[16,2048]{1,0:T(8,128)(2,1)S(1)}, bf16[16,2048]{1,0:T(8,128)(2,1)S(1)}, u32[]{:S(2)}, u32[]{:S(2)}) %collective-permute-start.27) | collective-permute-done | bytes 65568 | tf_op jit(solution)/shard_map/ppermute | solution.py:262
  125.1 3.5 %collective-permute-start.6 = (bf16[256,1024]{1,0:T(8,128)(2,1)S(1)}, bf16[256,1024]{1,0:T(8,128)(2,1)S(1)}, u32[]{:S(2)}, u32[]{:S(2)}) collective-permute-start(bf16[256,1024]{1,0:T(8,128)(2,1)S(1)} %dynamic-slice_convert_fusion), channel_id=1, source_target_pairs={{0,1},{1,0},{2,3},{3,2},{4,5},{5,4},{6,7},{7,6},{8,9},{9,8},{10,11... | collective-permute-start | bytes 1572872 | tf_op jit(solution)/shard_map/ppermute | solution.py:219
  128.8 2.3 %shard_map.113 = bf16[4096,128]{1,0:T(8,128)(2,1)} custom-call(bf16[128,4096]{1,0:T(8,128)(2,1)S(1)} %copy-done.4, bf16[128,4096]{1,0:T(8,128)(2,1)S(1)} %collective-permute-done.10.refs_1_, bf16[128,4096]{1,0:T(8,128)(2,1)S(1)} %copy-done.2, bf16[128,4096]{1,0:T(8,128)(2,1)S(1)} %collective-permute-done.12.refs_3_, ...), custom_call_target="tpu_custom_call" | custom-call | flops 1073741824 | bytes 9437184 | tf_op jit(solution)/shard_map/pallas_call | solution.py:118
  131.1 9.0 %collective-permute-done.6 = bf16[256,1024]{1,0:T(8,128)(2,1)S(1)} collective-permute-done((bf16[256,1024]{1,0:T(8,128)(2,1)S(1)}, bf16[256,1024]{1,0:T(8,128)(2,1)S(1)}, u32[]{:S(2)}, u32[]{:S(2)}) %collective-permute-start.6) | collective-permute-done | bytes 524320 | tf_op jit(solution)/shard_map/ppermute | solution.py:219
  (150 shorter events, 41.3 us)
Async XLA Ops:
  7.2 88.9 %all-gather.2.cloned.1.call-start = ((), (), s32[]{:S(2)}) async-start(), calls=%async_computation | async-start | bytes 8650752 | tf_op jit(solution)/shard_map/all_gather | solution.py:171
  13.8 9.0 %collective-permute-start.2 = (bf16[32,2048]{1,0:T(8,128)(2,1)S(1)}, bf16[32,2048]{1,0:T(8,128)(2,1)S(1)}, u32[]{:S(2)}, u32[]{:S(2)}) collective-permute-start(bf16[32,2048]{1,0:T(8,128)(2,1)S(1)} %pad_maximum_fusion.6), channel_id=1, source_target_pairs={{0,3},{1,2},{2,1},{3,0},{4,7},{5,6},{6,5},{7,4},{8,11},{9,10},{10,... | collective-permute-start | bytes 393224 | tf_op jit(solution)/shard_map/ppermute | solution.py:62
  23.8 33.7 %collective-permute-start.11 = (bf16[4096,128]{1,0:T(8,128)(2,1)}, bf16[4096,128]{1,0:T(8,128)(2,1)}, u32[]{:S(2)}, u32[]{:S(2)}) collective-permute-start(bf16[4096,128]{1,0:T(8,128)(2,1)} %param.12), channel_id=1, source_target_pairs={{0,64},{64,0},{1,65},{65,1},{2,66},{66,2},{3,67},{67,3},{4,68},{68... | collective-permute-start | bytes 3145736 | tf_op jit(solution)/shard_map/ppermute | solution.py:182
  25.7 9.8 %collective-permute-start.7 = (bf16[32,4096]{1,0:T(8,128)(2,1)S(1)}, bf16[32,4096]{1,0:T(8,128)(2,1)S(1)}, u32[]{:S(2)}, u32[]{:S(2)}) collective-permute-start(bf16[32,4096]{1,0:T(8,128)(2,1)S(1)} %maximum_select_fusion.8), channel_id=1, source_target_pairs={{0,12},{1,13},{2,14},{3,15},{4,0},{5,1},{6,2},{7,3},{8,4},{9,5},{1... | collective-permute-start | bytes 786440 | tf_op jit(solution)/shard_map/ppermute | solution.py:62
  29.4 10.2 %collective-permute-start.9 = (bf16[32,4096]{1,0:T(8,128)(2,1)S(1)}, bf16[32,4096]{1,0:T(8,128)(2,1)S(1)}, u32[]{:S(2)}, u32[]{:S(2)}) collective-permute-start(bf16[32,4096]{1,0:T(8,128)(2,1)S(1)} %maximum_select_fusion.8), channel_id=1, source_target_pairs={{0,4},{1,5},{2,6},{3,7},{4,8},{5,9},{6,10},{7,11},{8,12},{9,13},{1... | collective-permute-start | bytes 786440 | tf_op jit(solution)/shard_map/ppermute | solution.py:62
  30.5 16.4 %collective-permute-start.15 = (bf16[128,2048]{1,0:T(8,128)(2,1)S(1)}, bf16[128,2048]{1,0:T(8,128)(2,1)S(1)}, u32[]{:S(2)}, u32[]{:S(2)}) collective-permute-start(bf16[128,2048]{1,0:T(8,128)(2,1)S(1)} %pad_maximum_fusion.2), channel_id=1, source_target_pairs={{0,1},{1,0},{2,3},{3,2},{4,5},{5,4},{6,7},{7,6},{8,9},{9,8},{10,11... | collective-permute-start | bytes 1572872 | tf_op jit(solution)/shard_map/ppermute | solution.py:186
  35.5 42.3 %collective-permute-start.14 = (bf16[128,2048]{1,0:T(8,128)(2,1)S(1)}, bf16[128,2048]{1,0:T(8,128)(2,1)S(1)}, u32[]{:S(2)}, u32[]{:S(2)}) collective-permute-start(bf16[128,2048]{1,0:T(8,128)(2,1)S(1)} %pad_maximum_fusion.1), channel_id=1, source_target_pairs={{0,64},{64,0},{1,65},{65,1},{2,66},{66,2},{3,67},{67,3},{4,68},{68... | collective-permute-start | bytes 1572872 | tf_op jit(solution)/shard_map/ppermute | solution.py:187
  36.7 20.7 %collective-permute-start.3 = (bf16[128,2048]{1,0:T(8,128)(2,1)S(1)}, bf16[128,2048]{1,0:T(8,128)(2,1)S(1)}, u32[]{:S(2)}, u32[]{:S(2)}) collective-permute-start(bf16[128,2048]{1,0:T(8,128)(2,1)S(1)} %constant_dynamic-slice_fusion.6), channel_id=1, source_target_pairs={{0,1},{1,0},{2,3},{3,2},{4,5},{5,4},{6,7},{7,6},{8,9},{9,8},{10,11... | collective-permute-start | bytes 1572872 | tf_op jit(solution)/shard_map/ppermute | solution.py:192
  39.7 23.4 %collective-permute-start.10 = (bf16[128,4096]{1,0:T(8,128)(2,1)S(1)}, bf16[128,4096]{1,0:T(8,128)(2,1)S(1)}, u32[]{:S(2)}, u32[]{:S(2)}) collective-permute-start(bf16[128,4096]{1,0:T(8,128)(2,1)S(1)} %constant_dynamic-update-slice_fusion.refs_0_), channel_id=1, source_target_pairs={{0,48},{1,49},{2,50},{3,51},{4,52},{5,53},{6,54},{7,55},{8,56},{9,... | collective-permute-start | bytes 3145736 | tf_op jit(solution)/shard_map/ppermute | solution.py:62
  46.9 23.3 %collective-permute-start.12 = (bf16[128,4096]{1,0:T(8,128)(2,1)S(1)}, bf16[128,4096]{1,0:T(8,128)(2,1)S(1)}, u32[]{:S(2)}, u32[]{:S(2)}) collective-permute-start(bf16[128,4096]{1,0:T(8,128)(2,1)S(1)} %constant_dynamic-update-slice_fusion.refs_0_), channel_id=1, source_target_pairs={{0,16},{1,17},{2,18},{3,19},{4,20},{5,21},{6,22},{7,23},{8,24},{9,... | collective-permute-start | bytes 3145736 | tf_op jit(solution)/shard_map/ppermute | solution.py:62
  57.5 20.6 %collective-permute-start.16 = (bf16[128,2048]{1,0:T(8,128)(2,1)S(1)}, bf16[128,2048]{1,0:T(8,128)(2,1)S(1)}, u32[]{:S(2)}, u32[]{:S(2)}) collective-permute-start(bf16[128,2048]{1,0:T(8,128)(2,1)S(1)} %collective-permute-done.15), channel_id=1, source_target_pairs={{0,64},{64,0},{1,65},{65,1},{2,66},{66,2},{3,67},{67,3},{4,68},{68... | collective-permute-start | bytes 1572872 | tf_op jit(solution)/shard_map/ppermute | solution.py:188
  73.1 27.2 %collective-permute-start.5 = (f32[256,2048]{1,0:T(8,128)}, f32[256,2048]{1,0:T(8,128)}, u32[]{:S(2)}, u32[]{:S(2)}) collective-permute-start(f32[256,2048]{1,0:T(8,128)} %fusion.6), channel_id=1, source_target_pairs={{0,64},{64,0},{1,65},{65,1},{2,66},{66,2},{3,67},{67,3},{4,68},{68... | collective-permute-start | bytes 6291464 | tf_op jit(solution)/shard_map/ppermute | solution.py:199
  73.1 13.1 %collective-permute-start.19 = (bf16[64,4096]{1,0:T(8,128)(2,1)S(1)}, bf16[64,4096]{1,0:T(8,128)(2,1)S(1)}, u32[]{:S(2)}, u32[]{:S(2)}) collective-permute-start(bf16[64,4096]{1,0:T(8,128)(2,1)S(1)} %slice.72), channel_id=1, source_target_pairs={{0,48},{1,49},{2,50},{3,51},{4,52},{5,53},{6,54},{7,55},{8,56},{9,... | collective-permute-start | bytes 1572872 | tf_op jit(solution)/shard_map/ppermute | solution.py:62
  77.8 10.6 %collective-permute-start.20 = (bf16[64,4096]{1,0:T(8,128)(2,1)S(1)}, bf16[64,4096]{1,0:T(8,128)(2,1)S(1)}, u32[]{:S(2)}, u32[]{:S(2)}) collective-permute-start(bf16[64,4096]{1,0:T(8,128)(2,1)S(1)} %slice.73), channel_id=1, source_target_pairs={{0,16},{1,17},{2,18},{3,19},{4,20},{5,21},{6,22},{7,23},{8,24},{9,... | collective-permute-start | bytes 1572872 | tf_op jit(solution)/shard_map/ppermute | solution.py:62
  81.8 21.4 %collective-permute-start.17 = (bf16[128,2048]{1,0:T(8,128)(2,1)}, bf16[128,2048]{1,0:T(8,128)(2,1)}, u32[]{:S(2)}, u32[]{:S(2)}) collective-permute-start(bf16[128,2048]{1,0:T(8,128)(2,1)} %get-tuple-element.25), channel_id=1, source_target_pairs={{0,16},{1,17},{2,18},{3,19},{4,20},{5,21},{6,22},{7,23},{8,24},{9,... | collective-permute-start | bytes 1572872 | tf_op jit(solution)/shard_map/ppermute | solution.py:62
  83.6 19.6 %collective-permute-start.18 = (bf16[128,2048]{1,0:T(8,128)(2,1)}, bf16[128,2048]{1,0:T(8,128)(2,1)}, u32[]{:S(2)}, u32[]{:S(2)}) collective-permute-start(bf16[128,2048]{1,0:T(8,128)(2,1)} %get-tuple-element.26), channel_id=1, source_target_pairs={{0,48},{1,49},{2,50},{3,51},{4,52},{5,53},{6,54},{7,55},{8,56},{9,... | collective-permute-start | bytes 1572872 | tf_op jit(solution)/shard_map/ppermute | solution.py:62
  96.1 11.0 %collective-permute-start.22 = (bf16[128,2048]{1,0:T(8,128)(2,1)}, bf16[128,2048]{1,0:T(8,128)(2,1)S(1)}, u32[]{:S(2)}, u32[]{:S(2)}) collective-permute-start(bf16[128,2048]{1,0:T(8,128)(2,1)} %convolution_convert_fusion.1), channel_id=1, source_target_pairs={{0,32},{1,33},{2,34},{3,35},{4,36},{5,37},{6,38},{7,39},{8,40},{9,... | collective-permute-start | bytes 1572872 | tf_op jit(solution)/shard_map/ppermute | solution.py:62
  98.4 30.3 %collective-permute-start.29 = (bf16[128,4096]{1,0:T(8,128)(2,1)S(1)}, bf16[128,4096]{1,0:T(8,128)(2,1)S(1)}, u32[]{:S(2)}, u32[]{:S(2)}) collective-permute-start(bf16[128,4096]{1,0:T(8,128)(2,1)S(1)} %copy-done.4), channel_id=1, source_target_pairs={{0,64},{64,0},{1,65},{65,1},{2,66},{66,2},{3,67},{67,3},{4,68},{68... | collective-permute-start | bytes 3145736 | tf_op jit(solution)/shard_map/ppermute | solution.py:265
  100.3 28.4 %collective-permute-start.30 = (bf16[128,4096]{1,0:T(8,128)(2,1)S(1)}, bf16[128,4096]{1,0:T(8,128)(2,1)S(1)}, u32[]{:S(2)}, u32[]{:S(2)}) collective-permute-start(bf16[128,4096]{1,0:T(8,128)(2,1)S(1)} %collective-permute-done.10.refs_1_), channel_id=1, source_target_pairs={{0,64},{64,0},{1,65},{65,1},{2,66},{66,2},{3,67},{67,3},{4,68},{68... | collective-permute-start | bytes 3145736 | tf_op jit(solution)/shard_map/ppermute | solution.py:265
  108.6 11.5 %collective-permute-start.23 = (bf16[32,2048]{1,0:T(8,128)(2,1)S(1)}, bf16[32,2048]{1,0:T(8,128)(2,1)S(1)}, u32[]{:S(2)}, u32[]{:S(2)}) collective-permute-start(bf16[32,2048]{1,0:T(8,128)(2,1)S(1)} %get-tuple-element.33), channel_id=1, source_target_pairs={{0,4},{1,5},{2,6},{3,7},{4,8},{5,9},{6,10},{7,11},{8,12},{9,13},{1... | collective-permute-start | bytes 393224 | tf_op jit(solution)/shard_map/ppermute | solution.py:62
  111.4 8.7 %collective-permute-start.24 = (bf16[32,2048]{1,0:T(8,128)(2,1)S(1)}, bf16[32,2048]{1,0:T(8,128)(2,1)S(1)}, u32[]{:S(2)}, u32[]{:S(2)}) collective-permute-start(bf16[32,2048]{1,0:T(8,128)(2,1)S(1)} %get-tuple-element.35), channel_id=1, source_target_pairs={{0,8},{1,9},{2,10},{3,11},{4,12},{5,13},{6,14},{7,15},{8,0},{9,1},... | collective-permute-start | bytes 393224 | tf_op jit(solution)/shard_map/ppermute | solution.py:62
  111.5 9.2 %collective-permute-start.25 = (bf16[32,2048]{1,0:T(8,128)(2,1)S(1)}, bf16[32,2048]{1,0:T(8,128)(2,1)S(1)}, u32[]{:S(2)}, u32[]{:S(2)}) collective-permute-start(bf16[32,2048]{1,0:T(8,128)(2,1)S(1)} %get-tuple-element.34), channel_id=1, source_target_pairs={{0,12},{1,13},{2,14},{3,15},{4,0},{5,1},{6,2},{7,3},{8,4},{9,5},{1... | collective-permute-start | bytes 393224 | tf_op jit(solution)/shard_map/ppermute | solution.py:62
  125.1 15.0 %collective-permute-start.6 = (bf16[256,1024]{1,0:T(8,128)(2,1)S(1)}, bf16[256,1024]{1,0:T(8,128)(2,1)S(1)}, u32[]{:S(2)}, u32[]{:S(2)}) collective-permute-start(bf16[256,1024]{1,0:T(8,128)(2,1)S(1)} %dynamic-slice_convert_fusion), channel_id=1, source_target_pairs={{0,1},{1,0},{2,3},{3,2},{4,5},{5,4},{6,7},{7,6},{8,9},{9,8},{10,11... | collective-permute-start | bytes 1572872 | tf_op jit(solution)/shard_map/ppermute | solution.py:219
  128.7 11.5 %collective-permute-start.28 = (f32[16,1024]{1,0:T(8,128)S(1)}, f32[16,1024]{1,0:T(8,128)S(1)}, u32[]{:S(2)}, u32[]{:S(2)}) collective-permute-start(f32[16,1024]{1,0:T(8,128)S(1)} %get-tuple-element.41), channel_id=1, source_target_pairs={{0,64},{64,0},{1,65},{65,1},{2,66},{66,2},{3,67},{67,3},{4,68},{68... | collective-permute-start | bytes 196616 | tf_op jit(solution)/shard_map/ppermute | solution.py:267
  (33 other events, 350.7 us)
Sparse Core Ops, SparseCore 0:
  23.9 58.6 all-gather.1
